TPU v7x, 128 devices: a whole 4x4x4 slice. The times are simulated.
128 devices in a mesh: dp: 8 (over y, core), tensor: 16 (over x, z).
Axes of the slice: x: 4, y: 4, z: 4, core: 2. Of those that a mesh axis runs over, the one named last changes fastest.
Arguments:
- gradient: bfloat16 [4096, 14336], P('dp', 'tensor'), may hold values from -8000 to 8000
- block_owner: int32 [224], replicated, may hold values from 0 to 255, as said below
- tile_block: int32 [8, 112], replicated, may hold values from 0 to 223, as said below
- fast_weight: float32 [4096, 14336], P('dp', 'tensor'), may hold values from -6 to 6
- slow_flat: float32 [4096, 14336], P(('dp', 'tensor')), may hold values from -6 to 6
- left_stat: float32 [256, 512, 512], P(('dp', 'tensor')), may hold values from -6 to 6
- right_stat: float32 [256, 512, 512], P(('dp', 'tensor')), may hold values from -6 to 6
- left_basis: bfloat16 [256, 512, 512], P(('dp', 'tensor')), may hold values from -0.25 to 0.25
- right_basis: bfloat16 [256, 512, 512], P(('dp', 'tensor')), may hold values from -0.25 to 0.25
- first_moment: float32 [256, 512, 512], P(('dp', 'tensor')), may hold values from -3 to 3
- second_moment: float32 [256, 512, 512], P(('dp', 'tensor')), may hold values from 0.05 to 0.5
Outputs:
- fast_new: float32 [4096, 14336], P('dp', 'tensor')
- slow_new: float32 [4096, 14336], P(('dp', 'tensor'))
- left_new: float32 [256, 512, 512], P(('dp', 'tensor'))
- right_new: float32 [256, 512, 512], P(('dp', 'tensor'))
- moment_new: float32 [256, 512, 512], P(('dp', 'tensor'))
- second_new: float32 [256, 512, 512], P(('dp', 'tensor'))
Inputs may be any that keep to these rules, and one draw needn't show every extreme that they name: `tile_block`: entry [r, g] is the number of the block that tile g of block row r (columns g * 128 to g * 128 + 127) belongs to, one of r * (28) to r * 28 + 14336 // 512 - 1. Each such block has 4 tiles, which lie in the columns of different tensor indices. In each row the tensor indices fall into groups of 4, and every block takes one tile from each member of one group. `block_owner`: entry b is the slot d * 2 + k of block b's owner, where d = (dp index) * (number of tensor indices) + (tensor index) and k is 0 or 1; the owner's dp index is the block's row. No slot is named twice, every device owns one or two blocks, and a device's two blocks come from different groups.
All inputs are finite; a program needn't handle non-finite values.
Results may differ from a plain program's by a relative error of at most 0.00095.
Values may be sent and summed in bfloat16 or wider, within the bound.
No kernel may reach another device: no remote copies, remote signals or barrier semaphores. Data moves between devices by JAX's collectives and lax.ppermute only.
A program may use at most 128 MiB of HBM per device.

v0:
```python
import functools

import jax
import jax.numpy as jnp
from jax import lax
from jax.sharding import Mesh
from jax.sharding import PartitionSpec as P

TENSOR = ("tensor_0", "tensor_1")
DP = ("dp_0", "dp_1")
DP_TENSOR = ("dp_0", "dp_1", "tensor_0", "tensor_1")


BETA_STAT = 0.95
BETA_ONE = 0.9
BETA_TWO = 0.95
ADAM_EPS = 1e-08
STEP_RATE = 0.1
PULL_RATE = 0.5
CLIP_RMS = 0.5
HIGHEST = lax.Precision.HIGHEST


def over_axes(shard, axes):
    return functools.reduce(lax.psum, axes, shard)


def soap_block(
    grad_block, factor, left_stat, right_stat, left_basis, right_basis, first_moment, second_moment
):
    gram_left = jnp.dot(grad_block, grad_block.T, preferred_element_type=jnp.float32)
    gram_right = jnp.dot(grad_block.T, grad_block, preferred_element_type=jnp.float32)
    squared = factor * factor
    left_next = BETA_STAT * left_stat + (1.0 - BETA_STAT) * squared * gram_left
    right_next = BETA_STAT * right_stat + (1.0 - BETA_STAT) * squared * gram_right
    left_wide = left_basis.astype(jnp.float32)
    right_wide = right_basis.astype(jnp.float32)
    half_rotated = jnp.dot(left_basis.T, grad_block, preferred_element_type=jnp.float32)
    rotated = factor * jnp.dot(half_rotated, right_wide, precision=HIGHEST)
    moment_next = BETA_ONE * first_moment + (1.0 - BETA_ONE) * factor * grad_block.astype(
        jnp.float32
    )
    second_next = BETA_TWO * second_moment + (1.0 - BETA_TWO) * rotated * rotated
    moment_turned = jnp.dot(
        jnp.dot(left_wide.T, moment_next, precision=HIGHEST), right_wide, precision=HIGHEST
    )
    direction = moment_turned / (jnp.sqrt(second_next) + ADAM_EPS)
    update = jnp.dot(
        jnp.dot(left_wide, direction, precision=HIGHEST), right_wide.T, precision=HIGHEST
    )
    return (left_next, right_next, moment_next, second_next, update.astype(jnp.bfloat16))


def on_device(
    gradient,
    block_owner,
    tile_block,
    fast_weight,
    slow_flat,
    left_stat,
    right_stat,
    left_basis,
    right_basis,
    first_moment,
    second_moment,
):
    block_size = left_stat.shape[1]
    slot_count = left_stat.shape[0]
    row_count, shard_cols = gradient.shape
    tensor_size = lax.axis_size(TENSOR)
    column = lax.axis_index(TENSOR)
    dp_index = lax.axis_index(DP)
    tile_count = tile_block.shape[1]
    tile_width = shard_cols * tensor_size // tile_count
    shard_tiles = shard_cols // tile_width
    per_block = block_size // tile_width
    total_count = row_count * shard_cols * lax.axis_size(DP) * tensor_size
    wide_grad = gradient.astype(jnp.float32)
    square_sum = over_axes(jnp.sum(wide_grad * wide_grad), DP_TENSOR)
    factor = CLIP_RMS / jnp.sqrt(square_sum / total_count + 1e-06)
    numbers = jnp.arange(block_owner.shape[0], dtype=jnp.int32)
    peer_ids = jnp.arange(tensor_size, dtype=jnp.int32)
    positions = jnp.arange(per_block, dtype=jnp.int32)
    row_tiles = lax.dynamic_index_in_dim(tile_block, dp_index, 0, keepdims=False)
    peer_tiles = row_tiles.reshape(tensor_size, shard_tiles)
    my_blocks = lax.dynamic_index_in_dim(peer_tiles, column, 0, keepdims=False)
    owner_slot = jnp.sum(
        jnp.where(my_blocks[:, None] == numbers[None, :], block_owner[None, :], 0), axis=1
    )
    target = owner_slot // slot_count % tensor_size
    send_map = (peer_ids[:, None] == target[None, :]).astype(jnp.bfloat16)
    tile_view = gradient.reshape(row_count, shard_tiles, tile_width)
    outgoing = jnp.einsum(
        "pi,bit->pbt", send_map, tile_view, preferred_element_type=jnp.float32
    ).astype(jnp.bfloat16)
    arrived = lax.all_to_all(outgoing, TENSOR, split_axis=0, concat_axis=0, tiled=True)
    slot_ids = (dp_index * tensor_size + column) * slot_count + jnp.arange(
        slot_count, dtype=jnp.int32
    )
    matches = block_owner[None, :] == slot_ids[:, None]
    present = jnp.any(matches, axis=1)
    owned_block = jnp.sum(jnp.where(matches, numbers[None, :], 0), axis=1)
    holders = (
        jnp.any(peer_tiles[None, :, :] == owned_block[:, None, None], axis=2) & present[:, None]
    )
    slot_rank = jnp.cumsum(holders.astype(jnp.int32), axis=1) - 1
    select = (holders[:, None, :] & (slot_rank[:, None, :] == positions[None, :, None])).astype(
        jnp.bfloat16
    )
    blocks = jnp.einsum(
        "kjp,pbt->kbjt", select, arrived, preferred_element_type=jnp.float32
    ).astype(jnp.bfloat16)
    blocks = blocks.reshape(slot_count, block_size, block_size)
    results = jax.vmap(soap_block, in_axes=(0, None, 0, 0, 0, 0, 0, 0))(
        blocks, factor, left_stat, right_stat, left_basis, right_basis, first_moment, second_moment
    )
    keep_mask = present[:, None, None]
    left_new = jnp.where(keep_mask, results[0], left_stat)
    right_new = jnp.where(keep_mask, results[1], right_stat)
    moment_new = jnp.where(keep_mask, results[2], first_moment)
    second_new = jnp.where(keep_mask, results[3], second_moment)
    update = jnp.where(keep_mask, results[4], jnp.zeros((), jnp.bfloat16))
    pieces = update.reshape(slot_count, block_size, per_block, tile_width)
    backward = jnp.einsum(
        "kjp,kbjt->pbt", select, pieces, preferred_element_type=jnp.float32
    ).astype(jnp.bfloat16)
    returned = lax.all_to_all(backward, TENSOR, split_axis=0, concat_axis=0, tiled=True)
    home_update = jnp.einsum(
        "pi,pbt->bit", send_map, returned, preferred_element_type=jnp.float32
    ).reshape(row_count, shard_cols)
    fast_new = fast_weight - STEP_RATE * home_update
    flat_fast = lax.all_to_all(fast_new, TENSOR, split_axis=0, concat_axis=1, tiled=True)
    slow_new = slow_flat + PULL_RATE * (flat_fast - slow_flat)
    return (fast_new, slow_new, left_new, right_new, moment_new, second_new)


def solution(mesh):
    torus = Mesh(mesh.devices.reshape(4, 2, 4, 4), ("dp_0", "dp_1", "tensor_0", "tensor_1"))
    return jax.shard_map(
        on_device,
        mesh=torus,
        in_specs=(
            P(DP, TENSOR),
            P(),
            P(),
            P(DP, TENSOR),
            P(DP_TENSOR, None),
            P(DP_TENSOR, None, None),
            P(DP_TENSOR, None, None),
            P(DP_TENSOR, None, None),
            P(DP_TENSOR, None, None),
            P(DP_TENSOR, None, None),
            P(DP_TENSOR, None, None),
        ),
        out_specs=(
            P(DP, TENSOR),
            P(DP_TENSOR, None),
            P(DP_TENSOR, None, None),
            P(DP_TENSOR, None, None),
            P(DP_TENSOR, None, None),
            P(DP_TENSOR, None, None),
        ),
        check_vma=False,
    )
```

profile of v0, /device:TPU:0, one launch (start us, length us, event | category | flops | bytes accessed | tf_op | source)
XLA Modules:
  0.0 161.7 jit_solution(13364469936822803290)
XLA Ops:
  0.6 0.0 copy-start
  0.7 0.8 dynamic-slice_reduce_fusion
  1.5 0.1 eq.36
  1.6 0.9 select_reduce_fusion
  2.4 1.5 copy.96
  3.9 0.8 copy.97
  4.7 0.9 convolution_convert_fusion
  5.5 1.9 %copy.98 = bf16[16,512,128]{2,1,0:T(8,128)(2,1)} copy(bf16[16,512,128]{2,0,1:T(8,128)(2,1)S(1)} %convolution_convert_fusion) | data formatting | bytes 4194304 | tf_op jit(solution)/shard_map/convert_element_type | solution.py:95
  7.4 8.1 %all-to-all-start = ((bf16[16,512,128]{2,1,0:T(8,128)(2,1)}), bf16[16,512,128]{2,1,0:T(8,128)(2,1)S(1)}, u32[]{:S(2)}, u32[]{:S(2)}) async-start(bf16[16,512,128]{2,1,0:T(8,128)(2,1)} %copy.98), calls=%async_computation | async-start | bytes 4194304 | tf_op jit(solution)/shard_map/all_to_all | solution.py:96
  15.5 2.3 %multiply_reduce_fusion = f32[]{:T(128)} fusion(bf16[512,896]{1,0:T(8,128)(2,1)} %param.11), kind=kLoop, calls=%fused_computation.20 | loop fusion | flops 1376255 | bytes 917508 | tf_op jit(solution)/shard_map/reduce_sum | solution.py:79
  17.8 11.3 %psum.28 = f32[]{:T(128)} all-reduce(f32[]{:T(128)} %multiply_reduce_fusion), channel_id=1, replica_groups=mesh['dp_0'=4,'dp_1'=2,'tensor_0'=4,'tensor_1'=4] {'dp_0'}, use_global_device_ids=true, to_apply=%region_5.6 | all-reduce | flops 1 | bytes 8 | tf_op jit(solution)/shard_map/psum | solution.py:25
  29.1 3.1 %psum.29 = f32[]{:T(128)} all-reduce(f32[]{:T(128)} %psum.28), channel_id=1, replica_groups=mesh['dp_0'=4,'dp_1'=2,'tensor_0'=4,'tensor_1'=4] {'dp_1'}, use_global_device_ids=true, to_apply=%region_6.7 | all-reduce | flops 1 | bytes 8 | tf_op jit(solution)/shard_map/psum | solution.py:25
  32.2 12.7 %psum.30 = f32[]{:T(128)} all-reduce(f32[]{:T(128)} %psum.29), channel_id=1, replica_groups=mesh['dp_0'=4,'dp_1'=2,'tensor_0'=4,'tensor_1'=4] {'tensor_0'}, use_global_device_ids=true, to_apply=%region_7.8 | all-reduce | flops 1 | bytes 8 | tf_op jit(solution)/shard_map/psum | solution.py:25
  44.9 11.5 %psum.31 = f32[]{:T(128)} all-reduce(f32[]{:T(128)} %psum.30), channel_id=1, replica_groups=mesh['dp_0'=4,'dp_1'=2,'tensor_0'=4,'tensor_1'=4] {'tensor_1'}, use_global_device_ids=true, to_apply=%region_8.9 | all-reduce | flops 1 | bytes 8 | tf_op jit(solution)/shard_map/psum | solution.py:25
  56.4 0.1 copy.95
  56.5 0.2 fusion.34
  56.7 0.1 compare_reduce_fusion
  56.8 0.2 compare_reduce_fusion.1
  57.0 0.1 fusion.44
  57.1 0.2 reduce_window_sum.11
  58.0 2.4 %fusion.17 = bf16[2,512,4,128]{3,2,0,1:T(4,128)(2,1)} fusion(bf16[16,512,128,1]{2,1,0,3:T(8,128)(2,1)S(1)} %bitcast.45, s32[2,16]{1,0:T(2,128)S(1)} %broadcast_add_fusion, pred[2,16]{1,0:T(4,128)(4,1)S(1)} %get-tuple-element.37), kind=kOutput, calls=%fused_computation.24 | convolution fusion | flops 17301760 | bytes 3145888 | tf_op jit(solution)/shard_map/kjp,pbt->kbjt/dot_general | solution.py:110
  60.4 1.5 reshape.102
  61.8 1.6 %copy.103 = bf16[2,512,512]{1,2,0:T(8,128)(2,1)S(1)} copy(bf16[2,512,512]{2,0,1:T(2,128)(2,1)S(1)} %reshape.102) | data formatting | bytes 2097152 | tf_op jit(solution)/shard_map/reshape | solution.py:113
  63.5 0.0 copy-start.3
  63.5 2.1 %fusion.46 = f32[2,512,512]{1,2,0:T(8,128)S(1)} fusion(bf16[2,512,512]{1,2,0:T(8,128)(2,1)S(1)} %copy.103, bf16[2,512,512]{2,1,0:T(8,128)(2,1)} %param.18), kind=kOutput, calls=%fused_computation.67 | convolution fusion | flops 536870912 | bytes 4194304 | tf_op jit(solution)/shard_map/vmap()/dot_general | solution.py:38
  65.6 0.0 copy-done.3
  65.7 2.2 %fusion.10 = f32[2,512,512]{1,2,0:T(8,128)S(1)} fusion(bf16[2,512,512]{2,1,0:T(8,128)(2,1)S(1)} %copy-done.3, f32[2,512,512]{2,1,0:T(8,128)S(1)} %copy-done.2, f32[]{:T(128)S(6)} %mul.96, bf16[2,512,512]{2,0,1:T(2,128)(2,1)S(1)} %reshape.102), kind=kOutput, calls=%fused_computation.16 | convolution fusion | flops 3223322624 | bytes 6291460 | tf_op jit(solution)/shard_map/vmap()/dot_general | solution.py:45
  67.9 1.8 %fusion.45 = f32[2,512,512]{2,1,0:T(8,128)S(1)} fusion(f32[2,512,512]{1,2,0:T(8,128)S(1)} %fusion.10, bf16[2,512,512]{2,1,0:T(8,128)(2,1)S(1)} %copy-done), kind=kOutput, calls=%fused_computation.66 | convolution fusion | flops 3221225472 | bytes 5242880 | tf_op jit(solution)/shard_map/vmap()/dot_general | solution.py:44
  69.7 4.1 %broadcast_select_fusion = (f32[2,512,512]{2,1,0:T(8,128)}, f32[2,512,512]{2,1,0:T(8,128)}, f32[2,512,512]{2,1,0:T(8,128)S(1)}) fusion(f32[2,512,512]{2,1,0:T(8,128)S(1)} %copy-done.5, pred[2]{0:T(512)(128)(4,1)S(1)} %compare_reduce_fusion.1, f32[2,512,512]{2,1,0:T(8,128)S(1)} %copy-done.2, bf16[2,512,512]{2,0,1:T(2,128)(2,1)S(1)} %reshape.102, ...), kind=kOutput, calls=%fused_computation.28 | convolution fusion | flops 3226992640 | bytes 14680074 | tf_op jit(solution)/shard_map/vmap()/dot_general | solution.py:39
  73.8 4.0 %fusion.5 = f32[2,512,512]{2,1,0:T(8,128)S(1)} fusion(bf16[2,512,512]{2,1,0:T(8,128)(2,1)S(1)} %copy-done.3, f32[2,512,512]{2,1,0:T(8,128)S(1)} %fusion.45, f32[2,512,512]{2,1,0:T(8,128)S(1)} %get-tuple-element.40), kind=kOutput, calls=%fused_computation.10 | convolution fusion | flops 3222274048 | bytes 7340032 | tf_op jit(solution)/shard_map/vmap()/dot_general | solution.py:49
  77.8 4.8 %fusion.16 = bf16[2,512,512]{2,1,0:T(8,128)(2,1)} fusion(f32[2,512,512]{2,1,0:T(8,128)S(1)} %fusion.5, bf16[2,512,512]{2,1,0:T(8,128)(2,1)S(1)} %copy-done, pred[2]{0:T(512)(128)(4,1)S(1)} %compare_reduce_fusion.1), kind=kOutput, calls=%fused_computation.23 | convolution fusion | flops 3222274048 | bytes 4194306 | tf_op jit(solution)/shard_map/vmap()/dot_general | solution.py:48
  82.6 1.3 reshape.103
  84.0 1.1 bitcast_convert_fusion
  85.0 1.9 %copy.108 = bf16[16,512,128]{2,1,0:T(8,128)(2,1)} copy(bf16[16,512,128]{2,0,1:T(8,128)(2,1)S(1)} %bitcast_convert_fusion) | data formatting | bytes 4194304 | tf_op jit(solution)/shard_map/convert_element_type | solution.py:126
  86.9 4.4 %all-to-all-start.1 = ((bf16[16,512,128]{2,1,0:T(8,128)(2,1)}), bf16[16,512,128]{2,1,0:T(8,128)(2,1)}, u32[]{:S(2)}, u32[]{:S(2)}) async-start(bf16[16,512,128]{2,1,0:T(8,128)(2,1)} %copy.108), calls=%async_computation.1 | async-start | bytes 4194304 | tf_op jit(solution)/shard_map/all_to_all | solution.py:127
  91.3 2.7 %copy.111 = f32[512,896]{0,1:T(8,128)} copy(f32[512,896]{1,0:T(8,128)} %param.14) | data formatting | bytes 3670016 | tf_op args[3]
  94.0 22.4 %all-to-all-done.1 = bf16[16,512,128]{2,1,0:T(8,128)(2,1)} async-done(((bf16[16,512,128]{2,1,0:T(8,128)(2,1)}), bf16[16,512,128]{2,1,0:T(8,128)(2,1)}, u32[]{:S(2)}, u32[]{:S(2)}) %all-to-all-start.1) | async-done | bytes 2097184 | tf_op jit(solution)/shard_map/all_to_all | solution.py:127
  116.4 4.2 %multiply_bitcast_fusion = f32[512,7,128]{2,1,0:T(8,128)} fusion(bf16[16,512,128]{2,1,0:T(8,128)(2,1)} %all-to-all-done.1, s32[7]{0:T(128)S(1)} %and_select_fusion), kind=kOutput, calls=%fused_computation.9 | convolution fusion | flops 15138928 | bytes 3932188 | tf_op jit(solution)/shard_map/pi,pbt->bit/dot_general | solution.py:128
  120.7 2.8 %copy.110 = f32[512,7,128]{0,2,1:T(8,128)} copy(f32[512,7,128]{2,1,0:T(8,128)} %multiply_bitcast_fusion) | data formatting | bytes 3670016 | tf_op jit(solution)/shard_map/mul | solution.py:131
  123.5 3.7 %bitcast_subtract_fusion = f32[512,896]{0,1:T(8,128)} fusion(f32[512,896]{0,1:T(8,128)} %copy.111, f32[512,7,128]{0,2,1:T(8,128)} %copy.110), kind=kLoop, calls=%fused_computation.18 | loop fusion | flops 458752 | bytes 5505024 | tf_op jit(solution)/shard_map/sub | solution.py:131
  127.1 2.7 %copy.118 = f32[512,896]{1,0:T(8,128)} copy(f32[512,896]{0,1:T(8,128)} %bitcast_subtract_fusion) | data formatting | bytes 3670016
  129.9 4.4 %all-to-all-start.2 = ((f32[16,32,896]{2,1,0:T(8,128)}), f32[16,32,896]{2,1,0:T(8,128)}, u32[]{:S(2)}, u32[]{:S(2)}) async-start(f32[16,32,896]{2,1,0:T(8,128)} %bitcast.46), calls=%async_computation.2 | async-start | bytes 3670016 | tf_op jit(solution)/shard_map/all_to_all | solution.py:132
  134.3 0.0 copy-start.4
  134.3 3.9 %add_select_fusion.1 = f32[2,512,512]{2,1,0:T(8,128)} fusion(f32[2,512,512]{2,1,0:T(8,128)} %param.16, f32[]{:T(128)S(6)} %mul.113, pred[2]{0:T(512)(128)(4,1)S(1)} %compare_reduce_fusion.1, bf16[2,512,512]{2,0,1:T(2,128)(2,1)S(1)} %reshape.102), kind=kOutput, calls=%fused_computation.8 | convolution fusion | flops 538968064 | bytes 5242886 | tf_op jit(solution)/shard_map/vmap()/dot_general | solution.py:31
  138.2 2.1 %add_select_fusion = f32[2,512,512]{2,1,0:T(8,128)} fusion(f32[2,512,512]{2,1,0:T(8,128)S(1)} %copy-done.4, bf16[2,512,512]{1,2,0:T(8,128)(2,1)S(1)} %copy.103, f32[]{:T(128)S(6)} %mul.113, pred[2]{0:T(512)(128)(4,1)S(1)} %compare_reduce_fusion.1, bf16[2,512,512]{2,0,1:T(2,128)(2,1)S(1)} %reshape.102), kind=kOutput, calls=%fused_computation.7 | convolution fusion | flops 538968064 | bytes 6291462 | tf_op jit(solution)/shard_map/vmap()/dot_general | solution.py:32
  140.3 18.2 %all-to-all-done.2 = f32[16,32,896]{2,1,0:T(8,128)} async-done(((f32[16,32,896]{2,1,0:T(8,128)}), f32[16,32,896]{2,1,0:T(8,128)}, u32[]{:S(2)}, u32[]{:S(2)}) %all-to-all-start.2) | async-done | bytes 1835040 | tf_op jit(solution)/shard_map/all_to_all | solution.py:132
  158.5 1.6 %copy.128 = f32[16,4,8,896]{3,2,0,1:T(8,128)S(1)} copy(f32[16,4,8,896]{3,2,1,0:T(8,128)} %bitcast.16) | data formatting | bytes 3670016 | tf_op jit(solution)/shard_map/all_to_all | solution.py:132
  160.2 1.5 multiply_add_fusion.2
  (17 shorter events, 0.1 us)
Async XLA Ops:
  0.6 67.2 %copy-start = (bf16[2,512,512]{2,1,0:T(8,128)(2,1)S(1)}, bf16[2,512,512]{2,1,0:T(8,128)(2,1)}, u32[]{:S(2)}) copy-start(bf16[2,512,512]{2,1,0:T(8,128)(2,1)} %param.19) | copy-start | bytes 3145732
  7.4 49.1 %copy-start.7 = (s32[224]{0:T(256)S(1)}, s32[224]{0:T(256)}, u32[]{:S(2)}) copy-start(s32[224]{0:T(256)} %param.12) | copy-start | bytes 2692
  7.4 50.6 %all-to-all-start = ((bf16[16,512,128]{2,1,0:T(8,128)(2,1)}), bf16[16,512,128]{2,1,0:T(8,128)(2,1)S(1)}, u32[]{:S(2)}, u32[]{:S(2)}) async-start(bf16[16,512,128]{2,1,0:T(8,128)(2,1)} %copy.98), calls=%async_computation | async-start | bytes 4194304 | tf_op jit(solution)/shard_map/all_to_all | solution.py:96
  63.5 2.2 %copy-start.2 = (f32[2,512,512]{2,1,0:T(8,128)S(1)}, f32[2,512,512]{2,1,0:T(8,128)}, u32[]{:S(2)}) copy-start(f32[2,512,512]{2,1,0:T(8,128)} %param.20) | copy-start | bytes 6291460
  63.5 2.2 %copy-start.3 = (bf16[2,512,512]{2,1,0:T(8,128)(2,1)S(1)}, bf16[2,512,512]{2,1,0:T(8,128)(2,1)}, u32[]{:S(2)}) copy-start(bf16[2,512,512]{2,1,0:T(8,128)(2,1)} %param.18) | copy-start | bytes 3145732
  67.9 1.9 %copy-start.5 = (f32[2,512,512]{2,1,0:T(8,128)S(1)}, f32[2,512,512]{2,1,0:T(8,128)}, u32[]{:S(2)}) copy-start(f32[2,512,512]{2,1,0:T(8,128)} %param.21) | copy-start | bytes 6291460
  86.9 29.6 %all-to-all-start.1 = ((bf16[16,512,128]{2,1,0:T(8,128)(2,1)}), bf16[16,512,128]{2,1,0:T(8,128)(2,1)}, u32[]{:S(2)}, u32[]{:S(2)}) async-start(bf16[16,512,128]{2,1,0:T(8,128)(2,1)} %copy.108), calls=%async_computation.1 | async-start | bytes 4194304 | tf_op jit(solution)/shard_map/all_to_all | solution.py:127
  129.9 28.7 %all-to-all-start.2 = ((f32[16,32,896]{2,1,0:T(8,128)}), f32[16,32,896]{2,1,0:T(8,128)}, u32[]{:S(2)}, u32[]{:S(2)}) async-start(f32[16,32,896]{2,1,0:T(8,128)} %bitcast.46), calls=%async_computation.2 | async-start | bytes 3670016 | tf_op jit(solution)/shard_map/all_to_all | solution.py:132
  134.3 3.9 %copy-start.4 = (f32[2,512,512]{2,1,0:T(8,128)S(1)}, f32[2,512,512]{2,1,0:T(8,128)}, u32[]{:S(2)}) copy-start(f32[2,512,512]{2,1,0:T(8,128)} %param.17) | copy-start | bytes 6291460
  140.3 19.9 %copy-start.6 = (f32[32,14336]{1,0:T(8,128)S(1)}, f32[32,14336]{1,0:T(8,128)}, u32[]{:S(2)}) copy-start(f32[32,14336]{1,0:T(8,128)} %param.15) | copy-start | bytes 5505028
  160.2 1.5 copy-start.1
where the time goes:
time: 162 us
  waiting for transfers between devices  40.6 us (25%)
  blocking collectives  38.7 us (24%)
  matrix products  33.6 us (21%)
  local copies, waits for them, and re-layouts  21.2 us (13%)
  starting transfers between devices  17 us (10%)
  other arithmetic  9.03 us (6%)
    psum x4, blocking collectives, over_axes(): return functools.reduce(lax.psum, axes, shard)  38.7 us
    all_to_all x1, waiting for transfers between devices, on_device(): lax.all_to_all(backward, TENSOR, split_axis=0, concat_axis=0, tiled=True)  22.4 us
    all_to_all x1, waiting for transfers between devices, on_device(): lax.all_to_all(fast_new, TENSOR, split_axis=0, concat_axis=1, tiled=True)  18.2 us
    all_to_all x1, starting transfers between devices, on_device(): lax.all_to_all(outgoing, TENSOR, split_axis=0, concat_axis=0, tiled=True)  8.12 us
    unnamed x19, local copies, waits for them, and re-layouts  6.96 us
    dot_general x1, matrix products, soap_block(): jnp.dot(jnp.dot(left_wide, direction, precision=HIGHEST), right_wide.T, p...  4.81 us
    all_to_all x1, starting transfers between devices, on_device(): lax.all_to_all(backward, TENSOR, split_axis=0, concat_axis=0, tiled=True)  4.43 us
    all_to_all x1, starting transfers between devices, on_device(): lax.all_to_all(fast_new, TENSOR, split_axis=0, concat_axis=1, tiled=True)  4.41 us
  transfers between devices with their start and end apart: 3, of which 2 were waited for; matrix products, arithmetic and copies ran while one was open for 7% of the time, Pallas kernels for 0%

commit v1 on v0

v1 whole, which is shorter than its diff:
```python
import functools

import jax
import jax.numpy as jnp
from jax import lax
from jax.experimental import pallas as pl
from jax.experimental.pallas import tpu as pltpu
from jax.sharding import Mesh
from jax.sharding import PartitionSpec as P

TENSOR = ("tensor_0", "tensor_1")
DP = ("dp_0", "dp_1")
DP_TENSOR = ("dp_0", "dp_1", "tensor_0", "tensor_1")

BETA_STAT = 0.95
BETA_ONE = 0.9
BETA_TWO = 0.95
ADAM_EPS = 1e-08
STEP_RATE = 0.1
PULL_RATE = 0.5
CLIP_RMS = 0.5

F32 = jnp.float32
BF16 = jnp.bfloat16
TILE = 128
MIB = 1 << 20


def dot(a, b, dims=((1,), (0,))):
    return lax.dot_general(a, b, (dims, ((), ())), preferred_element_type=F32)


def halves(x):
    high = x.astype(BF16)
    return high, (x - high.astype(F32)).astype(BF16)


def params(mib, **kw):
    return pltpu.CompilerParams(vmem_limit_bytes=mib * MIB, **kw)


SMEM = pl.BlockSpec(memory_space=pltpu.SMEM)
ANY = pl.BlockSpec(memory_space=pl.ANY)


def pack_tiles(gradient, tile_block, block_owner, tensor_size):
    rows, cols = gradient.shape
    tiles = cols // TILE

    def body(tb, owner, grad, out, sems):
        row = lax.axis_index(DP)
        column = lax.axis_index(TENSOR)
        copies = []
        for i in range(tiles):
            slot = owner[tb[row, column * tiles + i]]
            target = (slot >> 1) & (tensor_size - 1)
            copy = pltpu.make_async_copy(
                grad.at[:, pl.ds(i * TILE, TILE)], out.at[target], sems.at[i]
            )
            copy.start()
            copies.append(copy)
        for copy in copies:
            copy.wait()

    return pl.pallas_call(
        body,
        out_shape=jax.ShapeDtypeStruct((tensor_size, rows, TILE), BF16),
        in_specs=[SMEM, SMEM, ANY],
        out_specs=ANY,
        scratch_shapes=[pltpu.SemaphoreType.DMA((tiles,))],
        compiler_params=params(1),
        name="pack",
    )(tile_block, block_owner, gradient)


def route_tables(tile_block, block_owner, tensor_size, shard_tiles, row_blocks, per_block):
    tile_count = tile_block.shape[1]

    def body(tb, owner, out, count):
        row = lax.axis_index(DP)
        mine = row * tensor_size + lax.axis_index(TENSOR)

        def clear(i, c):
            count[i] = 0
            return c

        lax.fori_loop(0, row_blocks, clear, 0)
        for i in range(tile_count, tile_count + 16):
            out[i] = 0

        def step(g, c):
            block = tb[row, g]
            local = block - row * row_blocks
            j = count[local]
            count[local] = j + 1
            slot = owner[block]
            out[g] = (((slot >> 1) & (tensor_size - 1)) * 2 + (slot & 1)) * per_block + j

            @pl.when((slot >> 1) == mine)
            def _():
                out[tile_count + (slot & 1) * per_block + j] = g // shard_tiles
                out[tile_count + 8 + (slot & 1)] = 1

            return c

        lax.fori_loop(0, tile_count, step, 0)

    return pl.pallas_call(
        body,
        out_shape=jax.ShapeDtypeStruct((128,), jnp.int32),
        in_specs=[SMEM, SMEM],
        out_specs=SMEM,
        scratch_shapes=[pltpu.SMEM((row_blocks,), jnp.int32)],
        compiler_params=params(1),
        name="tables",
    )(tile_block, block_owner)


def slot_spec(size):
    return pl.BlockSpec((1, size, size), lambda k, *_: (k, 0, 0))


def turn_moment(left, right, moment):
    slots, size, _ = left.shape

    def body(left_ref, right_ref, moment_ref, out, flipped):
        left_t = left_ref[0].T
        flipped[0] = left_t
        high, low = halves(moment_ref[0])
        half = dot(left_t, high) + dot(left_t, low)
        high, low = halves(half)
        out[0] = dot(high, right_ref[0]) + dot(low, right_ref[0])

    return pl.pallas_call(
        body,
        grid=(slots,),
        out_shape=(
            jax.ShapeDtypeStruct((slots, size, size), F32),
            jax.ShapeDtypeStruct((slots, size, size), BF16),
        ),
        in_specs=[slot_spec(size)] * 3,
        out_specs=(slot_spec(size), slot_spec(size)),
        compiler_params=params(20),
        name="turn_moment",
    )(left, right, moment)


def tile_specs(size, per_block, base):
    def spec(j):
        return pl.BlockSpec((1, size, TILE), lambda k, tab: (tab[base + k * per_block + j], 0, 0))

    return [spec(j) for j in range(per_block)]


def main_step(tables, factor, arrived, turned, left_t, left, right, second, base):
    slots, size, _ = left.shape
    per_block = size // TILE
    peers = arrived.shape[0]
    rows = size // peers

    def body(tab, factor_ref, *refs):
        tiles = refs[:per_block]
        turned_ref, left_t_ref, left_ref, right_ref, second_ref, second_out, send = refs[per_block:]
        k = pl.program_id(0)
        scale = factor_ref[0]
        grad = jnp.concatenate([t[0] for t in tiles], axis=1)
        right_wide = right_ref[0]
        high, low = halves(dot(left_t_ref[0], grad))
        rotated = scale * (dot(high, right_wide) + dot(low, right_wide))
        old = second_ref[0]
        new = BETA_TWO * old + (1.0 - BETA_TWO) * rotated * rotated
        second_out[0] = jnp.where(tab[base + 8 + k] == 1, new, old)
        direction = (BETA_ONE * turned_ref[0] + (1.0 - BETA_ONE) * rotated) / (
            jnp.sqrt(new) + ADAM_EPS
        )
        high, low = halves(direction)
        high, low = halves(dot(left_ref[0], high) + dot(left_ref[0], low))
        flip = ((1,), (1,))
        update = (dot(high, right_wide, flip) + dot(low, right_wide, flip)).astype(BF16)
        for j in range(per_block):
            send[:, 0, j] = update[:, j * TILE : (j + 1) * TILE].reshape(peers, rows, TILE)

    return pl.pallas_call(
        body,
        grid_spec=pltpu.PrefetchScalarGridSpec(
            num_scalar_prefetch=1,
            grid=(slots,),
            in_specs=[SMEM] + tile_specs(size, per_block, base) + [slot_spec(size)] * 5,
            out_specs=(
                slot_spec(size),
                pl.BlockSpec((peers, 1, per_block, rows, TILE), lambda k, *_: (0, k, 0, 0, 0)),
            ),
        ),
        out_shape=(
            jax.ShapeDtypeStruct((slots, size, size), F32),
            jax.ShapeDtypeStruct((peers, slots, per_block, rows, TILE), BF16),
        ),
        compiler_params=params(28),
        name="main_step",
    )(tables, factor, *([arrived] * per_block), turned, left_t, left, right, second)


def statistics(tables, factor, arrived, left_stat, right_stat, moment, base):
    slots, size, _ = left_stat.shape
    per_block = size // TILE

    def body(tab, factor_ref, *refs):
        tiles = refs[:per_block]
        left_ref, right_ref, moment_ref, left_out, right_out, moment_out = refs[per_block:]
        here = tab[base + 8 + pl.program_id(0)] == 1
        scale = factor_ref[0]
        squared = (1.0 - BETA_STAT) * (scale * scale)
        grad = jnp.concatenate([t[0] for t in tiles], axis=1)
        old = left_ref[0]
        new = BETA_STAT * old + squared * dot(grad, grad, ((1,), (1,)))
        left_out[0] = jnp.where(here, new, old)
        old = right_ref[0]
        new = BETA_STAT * old + squared * dot(grad.T, grad)
        right_out[0] = jnp.where(here, new, old)
        old = moment_ref[0]
        new = BETA_ONE * old + (1.0 - BETA_ONE) * scale * grad.astype(F32)
        moment_out[0] = jnp.where(here, new, old)

    return pl.pallas_call(
        body,
        grid_spec=pltpu.PrefetchScalarGridSpec(
            num_scalar_prefetch=1,
            grid=(slots,),
            in_specs=[SMEM] + tile_specs(size, per_block, base) + [slot_spec(size)] * 3,
            out_specs=(slot_spec(size),) * 3,
        ),
        out_shape=(jax.ShapeDtypeStruct((slots, size, size), F32),) * 3,
        compiler_params=params(28),
        name="statistics",
    )(tables, factor, *([arrived] * per_block), left_stat, right_stat, moment)


def place_tiles(tables, received, shard_tiles):
    places, rows, _ = received.shape
    tile_count = 112 if False else places // 8 * shard_tiles
    peers = tile_count // shard_tiles

    def body(tab, received_ref, out):
        def step(p, c):
            for i in range(shard_tiles):
                out[p, :, i * TILE : (i + 1) * TILE] = received_ref[tab[p * shard_tiles + i]]
            return c

        lax.fori_loop(0, peers, step, 0)

    vmem = pl.BlockSpec(memory_space=pltpu.VMEM)
    return pl.pallas_call(
        body,
        out_shape=jax.ShapeDtypeStruct((peers, rows, shard_tiles * TILE), BF16),
        in_specs=[SMEM, vmem],
        out_specs=vmem,
        compiler_params=params(6),
        name="place_tiles",
    )(tables, received)


def pull_slow(slow_flat, fast_rows, update_rows):
    peers, rows, width = fast_rows.shape

    def body(slow_ref, fast_ref, update_ref, out):
        slow = slow_ref[...]
        fast = fast_ref[0] - STEP_RATE * update_ref[0].astype(F32)
        out[...] = slow + PULL_RATE * (fast - slow)

    flat = pl.BlockSpec((rows, width), lambda p: (0, p))
    part = pl.BlockSpec((1, rows, width), lambda p: (p, 0, 0))
    return pl.pallas_call(
        body,
        grid=(peers,),
        out_shape=jax.ShapeDtypeStruct(slow_flat.shape, F32),
        in_specs=[flat, part, part],
        out_specs=flat,
        compiler_params=params(4),
        name="pull_slow",
    )(slow_flat, fast_rows, update_rows)


def exchange(x):
    return lax.all_to_all(x, TENSOR, split_axis=0, concat_axis=0, tiled=True)


def on_device(
    gradient,
    block_owner,
    tile_block,
    fast_weight,
    slow_flat,
    left_stat,
    right_stat,
    left_basis,
    right_basis,
    first_moment,
    second_moment,
):
    slots, size, _ = left_stat.shape
    row_count, shard_cols = gradient.shape
    peers = lax.axis_size(TENSOR)
    row_groups, tile_count = tile_block.shape
    shard_tiles = shard_cols // TILE
    per_block = size // TILE
    row_blocks = block_owner.shape[0] // row_groups
    total_count = row_count * shard_cols * lax.axis_size(DP) * peers

    outgoing = pack_tiles(gradient, tile_block, block_owner, peers)
    arrived = exchange(outgoing)
    tables = route_tables(tile_block, block_owner, peers, shard_tiles, row_blocks, per_block)
    wide = gradient.astype(F32)
    square_sum = functools.reduce(lax.psum, DP, jnp.sum(wide * wide))
    square_sum = exchange(jnp.full((peers, 8, TILE), square_sum, F32))
    square_sum = jnp.sum(square_sum[:, 0, 0])
    factor = (CLIP_RMS / jnp.sqrt(square_sum / total_count + 1e-06)).reshape(1)
    turned, left_t = turn_moment(left_basis, right_basis, first_moment)
    fast_rows = exchange(fast_weight.reshape(peers, row_count // peers, shard_cols))

    second_new, send = main_step(
        tables, factor, arrived, turned, left_t, left_basis, right_basis, second_moment, tile_count
    )
    received = exchange(send)
    left_new, right_new, moment_new = statistics(
        tables, factor, arrived, left_stat, right_stat, first_moment, tile_count
    )
    received = received.reshape(peers * slots * per_block, row_count // peers, TILE)
    update_rows = place_tiles(tables, received, shard_tiles)
    home = exchange(update_rows).reshape(row_count, shard_cols)
    slow_new = pull_slow(slow_flat, fast_rows, update_rows)
    fast_new = fast_weight - STEP_RATE * home.astype(F32)
    return (fast_new, slow_new, left_new, right_new, moment_new, second_new)


def solution(mesh):
    torus = Mesh(mesh.devices.reshape(4, 2, 4, 4), ("dp_0", "dp_1", "tensor_0", "tensor_1"))
    flat = P(DP_TENSOR, None)
    state = P(DP_TENSOR, None, None)
    return jax.shard_map(
        on_device,
        mesh=torus,
        in_specs=(P(DP, TENSOR), P(), P(), P(DP, TENSOR), flat) + (state,) * 6,
        out_specs=(P(DP, TENSOR), flat) + (state,) * 4,
        check_vma=False,
    )
```

time: 162 us -> 152 us (0.938)
  matrix products: 33.6 us -> 0 us
  Pallas kernels: 0 us -> 28.1 us
  blocking collectives: 38.7 us -> 33 us
  other arithmetic: 9.03 us -> 4.55 us
  starting transfers between devices: 17 us -> 20.4 us
    dot_general x12 -> x0, matrix products: 33.6 us -> none  [the longest x1 4.81 us: soap_block(): jnp.dot(jnp.dot(left_wide, direction, precision=HIGHEST), right_wide.T, p...]
    pallas_call x0 -> x7, Pallas kernels: none -> 28.1 us  [the longest x1 9.57 us: pull_slow(): pl.pallas_call(body, grid=(peers,), out_shape=jax.ShapeDtypeStruct(slow_f...]
    psum x4 -> x2, blocking collectives: 38.7 us -> 14.5 us  [on_device(): square_sum = functools.reduce(lax.psum, DP, jnp.sum(wide * wide))]
    all_to_all x0 -> x1, blocking collectives: none -> 18.5 us  [exchange(): return lax.all_to_all(x, TENSOR, split_axis=0, concat_axis=0, tiled=True)]
    unnamed x19 -> x40, local copies, waits for them, and re-layouts: 6.96 us -> 20.6 us
    reshape x4 -> x0, local copies, waits for them, and re-layouts: 5.2 us -> none  [the longest x2 3.1 us: on_device(): blocks = blocks.reshape(slot_count, block_size, block_size)]
    convert_element_type x2 -> x0, local copies, waits for them, and re-layouts: 3.72 us -> none  [the longest x1 1.86 us: on_device(): outgoing = jnp.einsum('pi,bit->pbt', send_map, tile_view, preferred_eleme...]
    all_to_all x3 -> x4, starting transfers between devices: 17 us -> 20.4 us  [exchange(): return lax.all_to_all(x, TENSOR, split_axis=0, concat_axis=0, tiled=True)]
  transfers between devices with their start and end apart: 3 -> 4, of which waited for: 2 -> 3; matrix products, arithmetic and copies ran while one was open for 7% -> 0% of each run, Pallas kernels for 0% -> 15%
where the time goes in v1:
time: 152 us; the launch traced here: 151 us
  waiting for transfers between devices  41.5 us (27%)
  blocking collectives  33 us (22%)
  Pallas kernels  28.1 us (18%)
  local copies, waits for them, and re-layouts  21.9 us (14%)
  starting transfers between devices  20.4 us (13%)
  other arithmetic  4.55 us (3%)
    all_to_all x4, waiting for transfers between devices, exchange(): return lax.all_to_all(x, TENSOR, split_axis=0, concat_axis=0, tiled=True)  41.5 us
    unnamed x40, local copies, waits for them, and re-layouts  20.6 us
    all_to_all x4, starting transfers between devices, exchange(): return lax.all_to_all(x, TENSOR, split_axis=0, concat_axis=0, tiled=True)  20.4 us
    all_to_all x1, blocking collectives, exchange(): return lax.all_to_all(x, TENSOR, split_axis=0, concat_axis=0, tiled=True)  18.5 us
    psum x2, blocking collectives, on_device(): square_sum = functools.reduce(lax.psum, DP, jnp.sum(wide * wide))  14.5 us
    pallas_call x1, Pallas kernels, pull_slow(): pl.pallas_call(body, grid=(peers,), out_shape=jax.ShapeDtypeStruct(slow_f...  9.57 us
    pallas_call x1, Pallas kernels, main_step(): pl.pallas_call(body, grid_spec=pltpu.PrefetchScalarGridSpec(num_scalar_pr...  6.13 us
    pallas_call x1, Pallas kernels, statistics(): pl.pallas_call(body, grid_spec=pltpu.PrefetchScalarGridSpec(num_scalar_pr...  3.73 us
  transfers between devices with their start and end apart: 4, of which 3 were waited for; matrix products, arithmetic and copies ran while one was open for 0% of the time, Pallas kernels for 15%

profile of v1, /device:TPU:0, one launch (start us, length us, event | category | flops | bytes accessed | tf_op | source)
XLA Modules:
  0.0 150.9 jit_solution(18220582483153318761)
XLA Ops:
  0.6 2.3 %multiply_reduce_fusion = f32[]{:T(128)} fusion(bf16[512,896]{1,0:T(8,128)(2,1)} %grad.1), kind=kLoop, calls=%fused_computation.2 | loop fusion | flops 1376255 | bytes 917508 | tf_op jit(solution)/shard_map/reduce_sum | solution.py:313
  2.9 11.5 %psum.14 = f32[]{:T(128)} all-reduce(f32[]{:T(128)} %multiply_reduce_fusion), channel_id=1, replica_groups=mesh['dp_0'=4,'dp_1'=2,'tensor_0'=4,'tensor_1'=4] {'dp_0'}, use_global_device_ids=true, to_apply=%region_1.0 | all-reduce | flops 1 | bytes 8 | tf_op jit(solution)/shard_map/psum | solution.py:313
  14.3 3.1 %psum.15 = f32[]{:T(128)} all-reduce(f32[]{:T(128)} %psum.14), channel_id=1, replica_groups=mesh['dp_0'=4,'dp_1'=2,'tensor_0'=4,'tensor_1'=4] {'dp_1'}, use_global_device_ids=true, to_apply=%region_2.0 | all-reduce | flops 1 | bytes 8 | tf_op jit(solution)/shard_map/psum | solution.py:313
  17.4 1.3 broadcast_in_dim.3
  18.7 7.9 %all-to-all-start = ((f32[16,8,128]{2,1,0:T(8,128)}), f32[16,8,128]{2,1,0:T(8,128)S(1)}, u32[]{:S(2)}, u32[]{:S(2)}) async-start(f32[16,8,128]{2,1,0:T(8,128)} %broadcast_in_dim.3), calls=%async_computation | async-start | bytes 131072 | tf_op jit(solution)/shard_map/all_to_all | solution.py:284
  26.6 0.0 copy-start.6
  26.6 1.2 copy-done.6
  27.8 0.7 copy-done.15
  28.5 0.7 copy-done.17
  29.1 0.9 pack.1
  30.0 0.0 copy-start
  30.1 1.3 copy-done
  31.4 2.9 %all-to-all-done = f32[16,8,128]{2,1,0:T(8,128)S(1)} async-done(((f32[16,8,128]{2,1,0:T(8,128)}), f32[16,8,128]{2,1,0:T(8,128)S(1)}, u32[]{:S(2)}, u32[]{:S(2)}) %all-to-all-start) | async-done | bytes 65568 | tf_op jit(solution)/shard_map/all_to_all | solution.py:284
  34.3 4.5 %all-to-all-start.1 = ((bf16[16,512,128]{2,1,0:T(8,128)(2,1)}), bf16[16,512,128]{2,1,0:T(8,128)(2,1)S(1)}, u32[]{:S(2)}, u32[]{:S(2)}) async-start(bf16[16,512,128]{2,1,0:T(8,128)(2,1)} %copy-done), calls=%async_computation.1 | async-start | bytes 4194304 | tf_op jit(solution)/shard_map/all_to_all | solution.py:284
  38.7 0.0 copy-done.16
  38.8 0.0 copy-done.18
  38.8 3.3 %tables.1.tab = s32[128]{0:T(128)S(1)} custom-call(s32[8,112]{1,0:T(8,128)S(1)} %copy-done.16, s32[224]{0:T(256)S(1)} %copy-done.18), custom_call_target="tpu_custom_call" | custom-call | tf_op jit(solution)/shard_map/tables/pallas_call | solution.py:108
  42.1 0.0 copy-done.3
  42.1 0.0 copy-start.1
  42.1 1.6 %copy-done.1 = f32[2,512,512]{2,1,0:T(8,128)S(1)} copy-done((f32[2,512,512]{2,1,0:T(8,128)S(1)}, f32[2,512,512]{2,1,0:T(8,128)}, u32[]{:S(2)}) %copy-start.1) | copy-done | bytes 2097176
  43.7 1.2 copy-done.4
  44.9 2.6 %turn_moment.1 = (f32[2,512,512]{2,1,0:T(8,128)S(1)}, bf16[2,512,512]{2,1,0:T(8,128)(2,1)S(1)}) custom-call(bf16[2,512,512]{2,1,0:T(8,128)(2,1)S(1)} %copy-done.3, bf16[2,512,512]{2,1,0:T(8,128)(2,1)S(1)} %copy-done.4, f32[2,512,512]{2,1,0:T(8,128)S(1)} %copy-done.1), custom_call_target="tpu_custom_call" | custom-call | tf_op jit(solution)/shard_map/turn_moment/pallas_call | solution.py:134
  47.6 0.0 copy-start.8
  47.6 1.3 copy-done.8
  48.9 1.0 copy-done.13
  49.9 0.6 slice_reduce_fusion
  51.2 17.6 %all-to-all-done.1.refs_0_.refs_1_.refs_2_.refs_3_ = bf16[16,512,128]{2,1,0:T(8,128)(2,1)S(1)} async-done(((bf16[16,512,128]{2,1,0:T(8,128)(2,1)}), bf16[16,512,128]{2,1,0:T(8,128)(2,1)S(1)}, u32[]{:S(2)}, u32[]{:S(2)}) %all-to-all-start.1) | async-done | bytes 2097184 | tf_op jit(solution)/shard_map/all_to_all | solution.py:284
  68.7 1.2 copy-done.5
  70.0 1.6 %copy-done.7 = f32[2,512,512]{2,1,0:T(8,128)S(1)} copy-done((f32[2,512,512]{2,1,0:T(8,128)S(1)}, f32[2,512,512]{2,1,0:T(8,128)}, u32[]{:S(2)}) %copy-start.7) | copy-done | bytes 2097176
  71.5 1.6 %copy-done.9 = f32[2,512,512]{2,1,0:T(8,128)S(1)} copy-done((f32[2,512,512]{2,1,0:T(8,128)S(1)}, f32[2,512,512]{2,1,0:T(8,128)}, u32[]{:S(2)}) %copy-start.9) | copy-done | bytes 2097176
  73.1 1.2 copy-done.14
  74.4 6.1 %main_step.1 = (f32[2,512,512]{2,1,0:T(8,128)}, bf16[16,2,4,32,128]{4,3,2,1,0:T(8,128)(2,1)S(1)}) custom-call(s32[128]{0:T(128)S(1)} %tables.1.tab, f32[1]{0:T(128)} %bitcast.factor_ref, bf16[16,512,128]{2,1,0:T(8,128)(2,1)S(1)} %all-to-all-done.1.refs_0_.refs_1_.refs_2_.refs_3_, bf16[16,512,128]{2,1,0:T(8,128)(2,1)S(1)} %all-to-all-done.1.refs_0_.refs_1_.refs_2_.refs_3_, ...), custom_call_target="tpu_custom_call" | custom-call | tf_op jit(solution)/shard_map/main_step/pallas_call | solution.py:183
  80.5 18.5 %all_to_all.25 = bf16[16,2,4,32,128]{4,3,2,1,0:T(8,128)(2,1)S(1)} all-to-all(bf16[16,2,4,32,128]{4,3,2,1,0:T(8,128)(2,1)S(1)} %get-tuple-element.15), channel_id=1, replica_groups=mesh['dp_0'=4,'dp_1'=2,'tensor_0'=4,'tensor_1'=4] {'tensor_0','tensor_1'}, dimensions={0} | all-to-all | bytes 2097152 | tf_op jit(solution)/shard_map/all_to_all | solution.py:284
  99.0 4.4 %all-to-all-start.4 = ((f32[16,32,896]{2,1,0:T(8,128)}), f32[16,32,896]{2,1,0:T(8,128)}, u32[]{:S(2)}, u32[]{:S(2)}) async-start(f32[16,32,896]{2,1,0:T(8,128)} %bitcast.6), calls=%async_computation.4 | async-start | bytes 3670016 | tf_op jit(solution)/shard_map/all_to_all | solution.py:284
  103.4 1.8 %place_tiles.1.update_ref = bf16[16,32,896]{2,1,0:T(8,128)(2,1)} custom-call(s32[128]{0:T(128)S(1)} %tables.1.tab, bf16[128,32,128]{2,1,0:T(8,128)(2,1)S(1)} %bitcast.5), custom_call_target="tpu_custom_call" | custom-call | tf_op jit(solution)/shard_map/place_tiles/pallas_call | solution.py:252
  105.2 21.1 %all-to-all-done.4.fast_ref = f32[16,32,896]{2,1,0:T(8,128)} async-done(((f32[16,32,896]{2,1,0:T(8,128)}), f32[16,32,896]{2,1,0:T(8,128)}, u32[]{:S(2)}, u32[]{:S(2)}) %all-to-all-start.4) | async-done | bytes 1835040 | tf_op jit(solution)/shard_map/all_to_all | solution.py:284
  126.3 3.6 %all-to-all-start.3 = ((bf16[16,32,896]{2,1,0:T(8,128)(2,1)}), bf16[16,32,896]{2,1,0:T(8,128)(2,1)S(1)}, u32[]{:S(2)}, u32[]{:S(2)}) async-start(bf16[16,32,896]{2,1,0:T(8,128)(2,1)} %place_tiles.1.update_ref), calls=%async_computation.3 | async-start | bytes 1835008 | tf_op jit(solution)/shard_map/all_to_all | solution.py:284
  129.9 0.0 copy-start.2
  129.9 1.6 %copy-done.2 = f32[2,512,512]{2,1,0:T(8,128)S(1)} copy-done((f32[2,512,512]{2,1,0:T(8,128)S(1)}, f32[2,512,512]{2,1,0:T(8,128)}, u32[]{:S(2)}) %copy-start.2) | copy-done | bytes 2097176
  131.5 1.6 %copy-done.10 = f32[2,512,512]{2,1,0:T(8,128)S(1)} copy-done((f32[2,512,512]{2,1,0:T(8,128)S(1)}, f32[2,512,512]{2,1,0:T(8,128)}, u32[]{:S(2)}) %copy-start.10) | copy-done | bytes 2097176
  133.1 1.6 %copy-done.11 = f32[2,512,512]{2,1,0:T(8,128)S(1)} copy-done((f32[2,512,512]{2,1,0:T(8,128)S(1)}, f32[2,512,512]{2,1,0:T(8,128)}, u32[]{:S(2)}) %copy-start.11) | copy-done | bytes 2097176
  134.7 3.7 %statistics.1 = (f32[2,512,512]{2,1,0:T(8,128)}, f32[2,512,512]{2,1,0:T(8,128)}, f32[2,512,512]{2,1,0:T(8,128)}) custom-call(s32[128]{0:T(128)S(1)} %tables.1.tab, f32[1]{0:T(128)} %bitcast.factor_ref, bf16[16,512,128]{2,1,0:T(8,128)(2,1)S(1)} %all-to-all-done.1.refs_0_.refs_1_.refs_2_.refs_3_, ...), custom_call_target="tpu_custom_call" | custom-call | tf_op jit(solution)/shard_map/statistics/pallas_call | solution.py:224
  138.4 0.0 copy-done.12
  138.4 9.6 %pull_slow.1 = f32[32,14336]{1,0:T(8,128)} custom-call(f32[32,14336]{1,0:T(8,128)S(1)} %copy-done.12, f32[16,32,896]{2,1,0:T(8,128)} %all-to-all-done.4.fast_ref, bf16[16,32,896]{2,1,0:T(8,128)(2,1)} %place_tiles.1.update_ref), custom_call_target="tpu_custom_call" | custom-call | tf_op jit(solution)/shard_map/pull_slow/pallas_call | solution.py:272
  148.0 0.0 all-to-all-done.3
  148.0 0.2 convert_multiply_fusion
  148.2 1.3 copy-done.19
  149.5 1.5 bitcast_subtract_fusion
  (15 shorter events, 0.0 us)
Async XLA Ops:
  18.7 15.6 %all-to-all-start = ((f32[16,8,128]{2,1,0:T(8,128)}), f32[16,8,128]{2,1,0:T(8,128)S(1)}, u32[]{:S(2)}, u32[]{:S(2)}) async-start(f32[16,8,128]{2,1,0:T(8,128)} %broadcast_in_dim.3), calls=%async_computation | async-start | bytes 131072 | tf_op jit(solution)/shard_map/all_to_all | solution.py:284
  26.6 1.2 copy-start.6
  27.8 0.7 copy-start.15
  28.5 0.7 copy-start.17
  30.0 1.3 copy-start
  31.4 7.4 %copy-start.16 = (s32[8,112]{1,0:T(8,128)S(1)}, s32[8,112]{1,0:T(8,128)}, u32[]{:S(2)}) copy-start(s32[8,112]{1,0:T(8,128)} %tb.3) | copy-start | bytes 10756
  31.4 7.4 %copy-start.18 = (s32[224]{0:T(256)S(1)}, s32[224]{0:T(256)}, u32[]{:S(2)}) copy-start(s32[224]{0:T(256)} %owner.3) | copy-start | bytes 2692
  31.4 10.7 %copy-start.3 = (bf16[2,512,512]{2,1,0:T(8,128)(2,1)S(1)}, bf16[2,512,512]{2,1,0:T(8,128)(2,1)}, u32[]{:S(2)}) copy-start(bf16[2,512,512]{2,1,0:T(8,128)(2,1)} %refs_6_.2) | copy-start | bytes 3145732
  34.3 34.5 %all-to-all-start.1 = ((bf16[16,512,128]{2,1,0:T(8,128)(2,1)}), bf16[16,512,128]{2,1,0:T(8,128)(2,1)S(1)}, u32[]{:S(2)}, u32[]{:S(2)}) async-start(bf16[16,512,128]{2,1,0:T(8,128)(2,1)} %copy-done), calls=%async_computation.1 | async-start | bytes 4194304 | tf_op jit(solution)/shard_map/all_to_all | solution.py:284
  42.1 1.6 %copy-start.1 = (f32[2,512,512]{2,1,0:T(8,128)S(1)}, f32[2,512,512]{2,1,0:T(8,128)}, u32[]{:S(2)}) copy-start(f32[2,512,512]{2,1,0:T(8,128)} %refs_6_.3) | copy-start | bytes 6291460
  43.7 1.2 copy-start.4
  47.6 1.3 copy-start.8
  48.9 1.0 copy-start.13
  68.7 1.2 copy-start.5
  70.0 1.6 %copy-start.7 = (f32[2,512,512]{2,1,0:T(8,128)S(1)}, f32[2,512,512]{2,1,0:T(8,128)}, u32[]{:S(2)}) copy-start(f32[2,512,512]{2,1,0:T(8,128)} %refs_8_.1) | copy-start | bytes 6291460
  71.5 1.6 %copy-start.9 = (f32[2,512,512]{2,1,0:T(8,128)S(1)}, f32[2,512,512]{2,1,0:T(8,128)}, u32[]{:S(2)}) copy-start(f32[2,512,512]{2,1,0:T(8,128)} %copy-done.8) | copy-start | bytes 6291460
  73.1 1.2 copy-start.14
  99.0 27.3 %all-to-all-start.4 = ((f32[16,32,896]{2,1,0:T(8,128)}), f32[16,32,896]{2,1,0:T(8,128)}, u32[]{:S(2)}, u32[]{:S(2)}) async-start(f32[16,32,896]{2,1,0:T(8,128)} %bitcast.6), calls=%async_computation.4 | async-start | bytes 3670016 | tf_op jit(solution)/shard_map/all_to_all | solution.py:284
  126.3 21.7 %all-to-all-start.3 = ((bf16[16,32,896]{2,1,0:T(8,128)(2,1)}), bf16[16,32,896]{2,1,0:T(8,128)(2,1)S(1)}, u32[]{:S(2)}, u32[]{:S(2)}) async-start(bf16[16,32,896]{2,1,0:T(8,128)(2,1)} %place_tiles.1.update_ref), calls=%async_computation.3 | async-start | bytes 1835008 | tf_op jit(solution)/shard_map/all_to_all | solution.py:284
  129.9 1.6 %copy-start.2 = (f32[2,512,512]{2,1,0:T(8,128)S(1)}, f32[2,512,512]{2,1,0:T(8,128)}, u32[]{:S(2)}) copy-start(f32[2,512,512]{2,1,0:T(8,128)} %refs_6_.3) | copy-start | bytes 6291460
  131.5 1.6 %copy-start.10 = (f32[2,512,512]{2,1,0:T(8,128)S(1)}, f32[2,512,512]{2,1,0:T(8,128)}, u32[]{:S(2)}) copy-start(f32[2,512,512]{2,1,0:T(8,128)} %refs_4_.1) | copy-start | bytes 6291460
  133.1 1.6 %copy-start.11 = (f32[2,512,512]{2,1,0:T(8,128)S(1)}, f32[2,512,512]{2,1,0:T(8,128)}, u32[]{:S(2)}) copy-start(f32[2,512,512]{2,1,0:T(8,128)} %refs_5_.1) | copy-start | bytes 6291460
  134.7 3.7 %copy-start.12 = (f32[32,14336]{1,0:T(8,128)S(1)}, f32[32,14336]{1,0:T(8,128)}, u32[]{:S(2)}) copy-start(f32[32,14336]{1,0:T(8,128)} %slow_ref.1) | copy-start | bytes 5505028
  148.0 1.5 copy-start.19

commit v2 on v1

v2 whole, which is shorter than its diff:
```python
import functools

import jax
import jax.numpy as jnp
from jax import lax
from jax.experimental import pallas as pl
from jax.experimental.pallas import tpu as pltpu
from jax.sharding import Mesh
from jax.sharding import PartitionSpec as P


TENSOR = ("tensor_0", "tensor_1")
DP = ("dp_0", "dp_1")
DP_TENSOR = ("dp_0", "dp_1", "tensor_0", "tensor_1")

BETA_STAT = 0.95
BETA_ONE = 0.9
BETA_TWO = 0.95
ADAM_EPS = 1e-08
STEP_RATE = 0.1
PULL_RATE = 0.5
CLIP_RMS = 0.5

F32 = jnp.float32
BF16 = jnp.bfloat16
TILE = 128
SPLIT = 320
MIB = 1 << 20


def dot(a, b, dims=((1,), (0,))):
    return lax.dot_general(a, b, (dims, ((), ())), preferred_element_type=F32)


def halves(x):
    high = x.astype(BF16)
    return high, (x - high.astype(F32)).astype(BF16)


SMALL = pltpu.CompilerParams(vmem_limit_bytes=8 * MIB)
PARAMS = pltpu.CompilerParams(vmem_limit_bytes=58 * MIB)


SMEM = pl.BlockSpec(memory_space=pltpu.SMEM)
VMEM = pl.BlockSpec(memory_space=pltpu.VMEM)
HBM = pl.BlockSpec(memory_space=pltpu.HBM)


def pack_tiles(gradient, tile_block, block_owner, peers, start, rows, parts=None):
    cols = gradient.shape[1]
    tiles = cols // TILE
    extra = 0 if parts is None else 32

    def body(tb, owner, grad, *refs):
        if extra:
            parts_ref, out, tile_v, addends, in_sems, out_sems = refs
        else:
            out, tile_v, in_sems, out_sems = refs
        row = lax.axis_index(DP)
        column = lax.axis_index(TENSOR)
        loads = []
        for i in range(tiles):
            loads.append(
                pltpu.make_async_copy(
                    grad.at[pl.ds(start, rows), pl.ds(i * TILE, TILE)], tile_v.at[i], in_sems.at[i]
                )
            )
            loads[-1].start()
        stores = []

        def store(source, target, n):
            stores.append(pltpu.make_async_copy(source, target, out_sems.at[n]))
            stores[-1].start()

        if extra:
            rest = parts_ref[...]
            pieces = []
            for _ in range(3):
                piece = rest.astype(BF16).astype(F32)
                pieces.append(piece)
                rest = rest - piece
            pieces.append(jnp.zeros_like(rest))
            addends[...] = jnp.concatenate(pieces, axis=0).astype(BF16)
            for p in range(peers):
                store(addends, out.at[p, pl.ds(rows, extra)], tiles + p)
        for i in range(tiles):
            slot = owner[tb[row, column * tiles + i]]
            target = (slot >> 1) & (peers - 1)
            loads[i].wait()
            store(tile_v.at[i], out.at[target, pl.ds(0, rows)], i)
        for copy in stores:
            copy.wait()

    return pl.pallas_call(
        body,
        out_shape=jax.ShapeDtypeStruct((peers, rows + extra, TILE), BF16),
        in_specs=[SMEM, SMEM, HBM] + ([VMEM] if extra else []),
        out_specs=HBM,
        scratch_shapes=[pltpu.VMEM((tiles, rows, TILE), BF16)]
        + ([pltpu.VMEM((extra, TILE), BF16)] if extra else [])
        + [
            pltpu.SemaphoreType.DMA((tiles,)),
            pltpu.SemaphoreType.DMA((tiles + (peers if extra else 0),)),
        ],
        compiler_params=PARAMS,
        name="pack",
    )(tile_block, block_owner, gradient, *([parts] if extra else []))


def route_tables(tile_block, block_owner, tensor_size, shard_tiles, row_blocks, per_block):
    tile_count = tile_block.shape[1]

    def body(tb, owner, out, count):
        row = lax.axis_index(DP)
        mine = row * tensor_size + lax.axis_index(TENSOR)

        def clear(i, c):
            count[i] = 0
            return c

        lax.fori_loop(0, row_blocks, clear, 0)
        for i in range(tile_count, tile_count + 16):
            out[i] = 0

        def step(g, c):
            block = tb[row, g]
            local = block - row * row_blocks
            j = count[local]
            count[local] = j + 1
            slot = owner[block]
            out[g] = (((slot >> 1) & (tensor_size - 1)) * 2 + (slot & 1)) * per_block + j

            @pl.when((slot >> 1) == mine)
            def _():
                out[tile_count + (slot & 1) * per_block + j] = g // shard_tiles
                out[tile_count + 8 + (slot & 1)] = 1

            return c

        lax.fori_loop(0, tile_count, step, 0)

    return pl.pallas_call(
        body,
        out_shape=jax.ShapeDtypeStruct((128,), jnp.int32),
        in_specs=[SMEM, SMEM],
        out_specs=SMEM,
        scratch_shapes=[pltpu.SMEM((row_blocks,), jnp.int32)],
        compiler_params=PARAMS,
        name="tables",
    )(tile_block, block_owner)


def square_parts(gradient):
    def body(grad, out):
        wide = grad[...].astype(F32)
        rows, cols = wide.shape
        part = jnp.sum((wide * wide).reshape(rows // 8, 8, cols), axis=0)
        out[...] = functools.reduce(
            jnp.add, [part[:, c : c + TILE] for c in range(0, cols, TILE)]
        )

    return pl.pallas_call(
        body,
        out_shape=jax.ShapeDtypeStruct((8, TILE), F32),
        in_specs=[VMEM],
        out_specs=VMEM,
        compiler_params=PARAMS,
        name="square_parts",
    )(gradient)


def clip_factor(parts, total_count):
    total = jnp.sum(jnp.sum(parts.astype(F32), axis=0), keepdims=True)
    return CLIP_RMS / jnp.sqrt(total / total_count + 1e-06)


def slot_spec(size):
    return pl.BlockSpec((1, size, size), lambda k, *_: (k, 0, 0))


def turn_moment(left, right, moment):
    slots, size, _ = left.shape

    def body(left_ref, right_ref, moment_ref, out, flipped):
        left_t = left_ref[0].T
        flipped[0] = left_t
        high, low = halves(moment_ref[0])
        half = dot(left_t, high) + dot(left_t, low)
        high, low = halves(half)
        out[0] = dot(high, right_ref[0]) + dot(low, right_ref[0])

    return pl.pallas_call(
        body,
        grid=(slots,),
        out_shape=(
            jax.ShapeDtypeStruct((slots, size, size), F32),
            jax.ShapeDtypeStruct((slots, size, size), BF16),
        ),
        in_specs=[slot_spec(size)] * 3,
        out_specs=(slot_spec(size), slot_spec(size)),
        compiler_params=PARAMS,
        name="turn_moment",
    )(left, right, moment)


def main_step(tables, first, rest, turned, left_t, left, right, second, base, total_count):
    slots, size, _ = left.shape
    per_block = size // TILE
    peers, split, _ = first.shape
    rows = size // peers
    names = 5 + 2 * per_block

    def body(
        tab, first_ref, rest_ref, turned_ref, left_t_ref, left_ref, right_ref, second_ref,
        second_out, send_out, grad_out, scale_out,
        grad_v, left_t_v, right_v, second_v, turned_v, left_v, new_v, send_v, parts_v, sems,
        out_sems,
    ):
        def loads(k):
            pairs = [(left_t_ref.at[k], left_t_v.at[k])]
            for j in range(per_block):
                source = tab[base + k * per_block + j]
                cols = pl.ds(j * TILE, TILE)
                pairs.append((first_ref.at[source], grad_v.at[k, pl.ds(0, split), cols]))
                pairs.append(
                    (
                        rest_ref.at[source, pl.ds(0, size - split)],
                        grad_v.at[k, pl.ds(split, size - split), cols],
                    )
                )
            pairs += [
                (right_ref.at[k], right_v.at[k]),
                (second_ref.at[k], second_v.at[k]),
                (turned_ref.at[k], turned_v.at[k]),
                (left_ref.at[k], left_v.at[k]),
            ]
            return [
                pltpu.make_async_copy(a, b, sems.at[k, n]) for n, (a, b) in enumerate(pairs)
            ]

        copies = [loads(k) for k in range(slots)]
        parts_copy = pltpu.make_async_copy(
            rest_ref.at[:, pl.ds(size - split, 32)], parts_v, out_sems.at[0, 3]
        )
        parts_copy.start()
        for group in copies:
            for copy in group:
                copy.start()
        parts_copy.wait()
        scale = clip_factor(parts_v[...], total_count)
        scale_out[...] = jnp.broadcast_to(scale, scale_out.shape)
        outs = []

        def emit(source, target, k, n):
            outs.append(pltpu.make_async_copy(source, target, out_sems.at[k, n]))
            outs[-1].start()

        for k in range(slots):
            wait = copies[k]
            for copy in wait[:-4]:
                copy.wait()
            emit(grad_v.at[k], grad_out.at[k], k, 2)
            high, low = halves(dot(left_t_v[k], grad_v[k]))
            wait[-4].wait()
            right_wide = right_v[k]
            rotated = scale * (dot(high, right_wide) + dot(low, right_wide))
            wait[-3].wait()
            old = second_v[k]
            new = BETA_TWO * old + (1.0 - BETA_TWO) * rotated * rotated
            new_v[k] = jnp.where(tab[base + 8 + k] == 1, new, old)
            emit(new_v.at[k], second_out.at[k], k, 0)
            wait[-2].wait()
            direction = (BETA_ONE * turned_v[k] + (1.0 - BETA_ONE) * rotated) / (
                jnp.sqrt(new) + ADAM_EPS
            )
            high, low = halves(direction)
            wait[-1].wait()
            high, low = halves(dot(left_v[k], high) + dot(left_v[k], low))
            flip = ((1,), (1,))
            update = (dot(high, right_wide, flip) + dot(low, right_wide, flip)).astype(BF16)
            width = per_block * rows
            for j in range(per_block):
                start = k * width + j * rows
                send_v[:, start : start + rows] = update[:, j * TILE : (j + 1) * TILE].reshape(
                    peers, rows, TILE
                )
            part = pl.ds(k * width, width)
            emit(send_v.at[:, part], send_out.at[:, part], k, 1)
        for out in outs:
            out.wait()

    square = (slots, size, size)
    return pl.pallas_call(
        body,
        out_shape=(
            jax.ShapeDtypeStruct(square, F32),
            jax.ShapeDtypeStruct((peers, slots * per_block * rows, TILE), BF16),
            jax.ShapeDtypeStruct(square, BF16),
            jax.ShapeDtypeStruct((8, TILE), F32),
        ),
        in_specs=[SMEM] + [HBM] * 7,
        out_specs=(HBM, HBM, HBM, VMEM),
        scratch_shapes=[pltpu.VMEM(square, BF16)] * 3
        + [pltpu.VMEM(square, F32)] * 2
        + [pltpu.VMEM(square, BF16), pltpu.VMEM(square, F32)]
        + [
            pltpu.VMEM((peers, slots * per_block * rows, TILE), BF16),
            pltpu.VMEM((peers, 32, TILE), BF16),
            pltpu.SemaphoreType.DMA((slots, names)),
            pltpu.SemaphoreType.DMA((slots, 4)),
        ],
        compiler_params=PARAMS,
        name="main_step",
    )(tables, first, rest, turned, left_t, left, right, second)


def statistics(tables, scale, grad, left_stat, right_stat, moment, base):
    slots, size, _ = left_stat.shape

    def body(tab, scale_ref, grad_ref, left_ref, right_ref, moment_ref, *outs):
        left_out, right_out, moment_out = outs
        here = tab[base + 8 + pl.program_id(0)] == 1
        scale = scale_ref[0:1, 0:1]
        squared = (1.0 - BETA_STAT) * (scale * scale)
        grad = grad_ref[0]
        old = left_ref[0]
        new = BETA_STAT * old + squared * dot(grad, grad, ((1,), (1,)))
        left_out[0] = jnp.where(here, new, old)
        old = right_ref[0]
        new = BETA_STAT * old + squared * dot(grad.T, grad)
        right_out[0] = jnp.where(here, new, old)
        old = moment_ref[0]
        new = BETA_ONE * old + (1.0 - BETA_ONE) * scale * grad.astype(F32)
        moment_out[0] = jnp.where(here, new, old)

    return pl.pallas_call(
        body,
        grid_spec=pltpu.PrefetchScalarGridSpec(
            num_scalar_prefetch=1,
            grid=(slots,),
            in_specs=[VMEM] + [slot_spec(size)] * 4,
            out_specs=(slot_spec(size),) * 3,
        ),
        out_shape=(jax.ShapeDtypeStruct((slots, size, size), F32),) * 3,
        compiler_params=PARAMS,
        name="statistics",
    )(tables, scale, grad, left_stat, right_stat, moment)


def place_tiles(tables, received, shard_tiles):
    places, rows, _ = received.shape
    peers = places // 8

    def body(tab, received_ref, out):
        def step(p, c):
            for i in range(shard_tiles):
                out[p, :, i * TILE : (i + 1) * TILE] = received_ref[tab[p * shard_tiles + i]]
            return c

        lax.fori_loop(0, peers, step, 0)

    return pl.pallas_call(
        body,
        out_shape=jax.ShapeDtypeStruct((peers, rows, shard_tiles * TILE), BF16),
        in_specs=[SMEM, VMEM],
        out_specs=VMEM,
        compiler_params=SMALL,
        name="place_tiles",
    )(tables, received)


def pull_slow(slow_flat, fast_rows, update_rows):
    peers, rows, width = fast_rows.shape
    step = 4

    def body(slow_ref, fast_ref, update_ref, out):
        for q in range(step):
            cols = slice(q * width, (q + 1) * width)
            slow = slow_ref[:, cols]
            fast = fast_ref[q] - STEP_RATE * update_ref[q].astype(F32)
            out[:, cols] = slow + PULL_RATE * (fast - slow)

    flat = pl.BlockSpec((rows, step * width), lambda p: (0, p))
    part = pl.BlockSpec((step, rows, width), lambda p: (p, 0, 0))
    return pl.pallas_call(
        body,
        grid=(peers // step,),
        out_shape=jax.ShapeDtypeStruct(slow_flat.shape, F32),
        in_specs=[flat, part, part],
        out_specs=flat,
        compiler_params=PARAMS,
        name="pull_slow",
    )(slow_flat, fast_rows, update_rows)


def exchange(x, axes=TENSOR):
    return lax.all_to_all(x, axes, split_axis=0, concat_axis=0, tiled=True)


def on_device(
    gradient,
    block_owner,
    tile_block,
    fast_weight,
    slow_flat,
    left_stat,
    right_stat,
    left_basis,
    right_basis,
    first_moment,
    second_moment,
):
    slots, size, _ = left_stat.shape
    row_count, shard_cols = gradient.shape
    peers = lax.axis_size(TENSOR)
    row_groups, tile_count = tile_block.shape
    shard_tiles = shard_cols // TILE
    per_block = size // TILE
    row_blocks = block_owner.shape[0] // row_groups
    total_count = row_count * shard_cols * lax.axis_size(DP) * peers

    first = pack_tiles(gradient, tile_block, block_owner, peers, 0, SPLIT)
    first = exchange(first)
    parts = square_parts(gradient)
    parts = functools.reduce(lax.psum, DP, parts)
    rest = pack_tiles(gradient, tile_block, block_owner, peers, SPLIT, size - SPLIT, parts)
    rest = exchange(rest)
    tables = route_tables(tile_block, block_owner, peers, shard_tiles, row_blocks, per_block)
    turned, left_t = turn_moment(left_basis, right_basis, first_moment)
    by_rows = (peers, row_count // peers, shard_cols)
    fast_half = fast_weight.reshape(by_rows).astype(jnp.float16)
    fast_rows = exchange(fast_half)
    second_new, send, grad, scale = main_step(
        tables, first, rest, turned, left_t, left_basis, right_basis, second_moment,
        tile_count, total_count,
    )
    received = exchange(send)
    left_new, right_new, moment_new = statistics(
        tables, scale, grad, left_stat, right_stat, first_moment, tile_count
    )
    received = received.reshape(peers * slots * per_block, row_count // peers, TILE)
    update_rows = place_tiles(tables, received, shard_tiles)
    home = exchange(update_rows)
    slow_new = pull_slow(slow_flat, fast_rows.astype(F32), update_rows)
    fast_new = fast_weight.reshape(by_rows) - STEP_RATE * home.astype(F32)
    fast_new = fast_new.reshape(row_count, shard_cols)
    return (fast_new, slow_new, left_new, right_new, moment_new, second_new)


def solution(mesh):
    torus = Mesh(mesh.devices.reshape(4, 2, 4, 4), ("dp_0", "dp_1", "tensor_0", "tensor_1"))
    flat = P(DP_TENSOR, None)
    state = P(DP_TENSOR, None, None)
    return jax.shard_map(
        on_device,
        mesh=torus,
        in_specs=(P(DP, TENSOR), P(), P(), P(DP, TENSOR), flat) + (state,) * 6,
        out_specs=(P(DP, TENSOR), flat) + (state,) * 4,
        check_vma=False,
    )
```

time: 152 us -> 138 us (0.908)
  local copies, waits for them, and re-layouts: 21.9 us -> 1.07 us
  blocking collectives: 33 us -> 14 us
  Pallas kernels: 28.1 us -> 40.8 us
  waiting for transfers between devices: 41.5 us -> 51.5 us
  starting transfers between devices: 20.4 us -> 23.3 us
    unnamed x40 -> x8, local copies, waits for them, and re-layouts: 20.6 us -> 1.07 us
    all_to_all x1 -> x0, blocking collectives: 18.5 us -> none  [exchange(): return lax.all_to_all(x, TENSOR, split_axis=0, concat_axis=0, tiled=True)]
    all_to_all x4 -> x5, waiting for transfers between devices: 41.5 us -> 51.5 us  [exchange(): return lax.all_to_all(x, axes, split_axis=0, concat_axis=0, tiled=True)]
    pallas_call x3 -> x5, Pallas kernels: 16.6 us -> 23.9 us  [the longest x1 12.4 us: main_step(): pl.pallas_call(body, out_shape=(jax.ShapeDtypeStruct(square, F32), jax.Sh...]
    convert_element_type x0 -> x2, other arithmetic: none -> 3.65 us  [the longest x1 2.61 us: on_device(): slow_new = pull_slow(slow_flat, fast_rows.astype(F32), update_rows)]
    all_to_all x4 -> x5, starting transfers between devices: 20.4 us -> 23.3 us  [exchange(): return lax.all_to_all(x, axes, split_axis=0, concat_axis=0, tiled=True)]
    pallas_call x1, Pallas kernels: 3.73 us -> 6.61 us  [statistics(): pl.pallas_call(body, grid_spec=pltpu.PrefetchScalarGridSpec(num_scalar_pr...]
    reduce_sum x2 -> x0, other arithmetic: 2.87 us -> none  [the longest x1 2.26 us: on_device(): square_sum = functools.reduce(lax.psum, DP, jnp.sum(wide * wide))]
  transfers between devices with their start and end apart: 4 -> 5, of which waited for: 3 -> 5; matrix products, arithmetic and copies ran while one was open for 0% -> 3% of each run, Pallas kernels for 15% -> 17%
where the time goes in v2:
time: 138 us; the launch traced here: 137 us
  waiting for transfers between devices  51.5 us (37%)
  Pallas kernels  40.8 us (30%)
  starting transfers between devices  23.3 us (17%)
  blocking collectives  14 us (10%)
  other arithmetic  5.15 us (4%)
    all_to_all x5, waiting for transfers between devices, exchange(): return lax.all_to_all(x, axes, split_axis=0, concat_axis=0, tiled=True)  51.5 us
    all_to_all x5, starting transfers between devices, exchange(): return lax.all_to_all(x, axes, split_axis=0, concat_axis=0, tiled=True)  23.3 us
    psum x2, blocking collectives, on_device(): parts = functools.reduce(lax.psum, DP, parts)  14 us
    pallas_call x1, Pallas kernels, main_step(): pl.pallas_call(body, out_shape=(jax.ShapeDtypeStruct(square, F32), jax.Sh...  12.4 us
    pallas_call x1, Pallas kernels, statistics(): pl.pallas_call(body, grid_spec=pltpu.PrefetchScalarGridSpec(num_scalar_pr...  6.61 us
    pallas_call x2, Pallas kernels, pack_tiles(): pl.pallas_call(body, out_shape=jax.ShapeDtypeStruct((peers, rows + extra,...  5.31 us
    pallas_call x1, Pallas kernels, turn_moment(): pl.pallas_call(body, grid=(slots,), out_shape=(jax.ShapeDtypeStruct((slot...  5.14 us
    pallas_call x1, Pallas kernels, pull_slow(): pl.pallas_call(body, grid=(peers // step,), out_shape=jax.ShapeDtypeStruc...  4.24 us
  transfers between devices with their start and end apart: 5, of which 5 were waited for; matrix products, arithmetic and copies ran while one was open for 3% of the time, Pallas kernels for 17%

profile of v2, /device:TPU:0, one launch (start us, length us, event | category | flops | bytes accessed | tf_op | source)
XLA Modules:
  0.0 136.7 jit_solution(3856139753971082574)
XLA Ops:
  0.6 1.9 %square_parts.1 = f32[8,128]{1,0:T(8,128)} custom-call(bf16[512,896]{1,0:T(8,128)(2,1)} %grad.5), custom_call_target="tpu_custom_call" | custom-call | tf_op jit(solution)/shard_map/square_parts/pallas_call | solution.py:162
  2.5 11.0 %psum.14 = f32[8,128]{1,0:T(8,128)S(1)} all-reduce(f32[8,128]{1,0:T(8,128)} %square_parts.1), channel_id=1, replica_groups=mesh['dp_0'=4,'dp_1'=2,'tensor_0'=4,'tensor_1'=4] {'dp_0'}, use_global_device_ids=true, to_apply=%region_0.0 | all-reduce | flops 1024 | bytes 8192 | tf_op jit(solution)/shard_map/psum | solution.py:425
  13.5 3.0 %psum.15.refs_0_ = f32[8,128]{1,0:T(8,128)} all-reduce(f32[8,128]{1,0:T(8,128)S(1)} %psum.14), channel_id=1, replica_groups=mesh['dp_0'=4,'dp_1'=2,'tensor_0'=4,'tensor_1'=4] {'dp_1'}, use_global_device_ids=true, to_apply=%region_1.0 | all-reduce | flops 1024 | bytes 8192 | tf_op jit(solution)/shard_map/psum | solution.py:425
  16.5 2.7 %pack.3 = bf16[16,224,128]{2,1,0:T(8,128)(2,1)} custom-call(s32[8,112]{1,0:T(8,128)} %tb.5, s32[224]{0:T(256)} %owner.5, bf16[512,896]{1,0:T(8,128)(2,1)} %grad.5, f32[8,128]{1,0:T(8,128)} %psum.15.refs_0_), custom_call_target="tpu_custom_call" | custom-call | tf_op jit(solution)/shard_map/pack/pallas_call | solution.py:94
  19.2 7.9 %all-to-all-start.1 = ((bf16[16,224,128]{2,1,0:T(8,128)(2,1)}), bf16[16,224,128]{2,1,0:T(8,128)(2,1)S(1)}, u32[]{:S(2)}, u32[]{:S(2)}) async-start(bf16[16,224,128]{2,1,0:T(8,128)(2,1)} %pack.3), calls=%async_computation.1 | async-start | bytes 1835008 | tf_op jit(solution)/shard_map/all_to_all | solution.py:397
  27.1 2.7 %pack.2 = bf16[16,320,128]{2,1,0:T(8,128)(2,1)} custom-call(s32[8,112]{1,0:T(8,128)} %tb.5, s32[224]{0:T(256)} %owner.5, bf16[512,896]{1,0:T(8,128)(2,1)} %grad.5), custom_call_target="tpu_custom_call" | custom-call | tf_op jit(solution)/shard_map/pack/pallas_call | solution.py:94
  29.7 13.9 %all-to-all-done.1.rest_ref = bf16[16,224,128]{2,1,0:T(8,128)(2,1)S(1)} async-done(((bf16[16,224,128]{2,1,0:T(8,128)(2,1)}), bf16[16,224,128]{2,1,0:T(8,128)(2,1)S(1)}, u32[]{:S(2)}, u32[]{:S(2)}) %all-to-all-start.1) | async-done | bytes 917536 | tf_op jit(solution)/shard_map/all_to_all | solution.py:397
  43.6 0.0 copy-start.3
  43.6 3.7 %all-to-all-start = ((bf16[16,320,128]{2,1,0:T(8,128)(2,1)}), bf16[16,320,128]{2,1,0:T(8,128)(2,1)S(1)}, u32[]{:S(2)}, u32[]{:S(2)}) async-start(bf16[16,320,128]{2,1,0:T(8,128)(2,1)} %pack.2), calls=%async_computation | async-start | bytes 2621440 | tf_op jit(solution)/shard_map/all_to_all | solution.py:397
  47.3 3.4 %tables.1.tab = s32[128]{0:T(128)} custom-call(s32[8,112]{1,0:T(8,128)} %tb.5, s32[224]{0:T(256)} %owner.5), custom_call_target="tpu_custom_call" | custom-call | tf_op jit(solution)/shard_map/tables/pallas_call | solution.py:142
  50.8 5.1 %turn_moment.1 = (f32[2,512,512]{2,1,0:T(8,128)}, bf16[2,512,512]{2,1,0:T(8,128)(2,1)}) custom-call(bf16[2,512,512]{2,1,0:T(8,128)(2,1)} %left_ref.4, bf16[2,512,512]{2,1,0:T(8,128)(2,1)} %right_ref.4, f32[2,512,512]{2,1,0:T(8,128)} %moment_ref.3), custom_call_target="tpu_custom_call" | custom-call | tf_op jit(solution)/shard_map/turn_moment/pallas_call | solution.py:192
  55.9 0.0 copy-done.3
  55.9 10.6 %all-to-all-done.first_ref = bf16[16,320,128]{2,1,0:T(8,128)(2,1)S(1)} async-done(((bf16[16,320,128]{2,1,0:T(8,128)(2,1)}), bf16[16,320,128]{2,1,0:T(8,128)(2,1)S(1)}, u32[]{:S(2)}, u32[]{:S(2)}) %all-to-all-start) | async-done | bytes 1310752 | tf_op jit(solution)/shard_map/all_to_all | solution.py:397
  66.5 0.0 copy-start.2
  66.5 1.1 copy-done.2
  67.5 12.4 %main_step.1 = (f32[2,512,512]{2,1,0:T(8,128)}, bf16[16,256,128]{2,1,0:T(8,128)(2,1)}, bf16[2,512,512]{2,1,0:T(8,128)(2,1)}, f32[8,128]{1,0:T(8,128)}) custom-call(s32[128]{0:T(128)} %tables.1.tab, bf16[16,320,128]{2,1,0:T(8,128)(2,1)} %copy-done.2, bf16[16,224,128]{2,1,0:T(8,128)(2,1)} %copy-done.3, f32[2,512,512]{2,1,0:T(8,128)} %get-tuple-element.15.turned_ref, ...), custom_call_target="tpu_custom_call" | custom-call | tf_op jit(solution)/shard_map/main_step/pallas_call | solution.py:293
  80.0 0.0 copy-start.1
  80.0 3.8 %all-to-all-start.2 = ((bf16[16,256,128]{2,1,0:T(8,128)(2,1)}), bf16[16,256,128]{2,1,0:T(8,128)(2,1)S(1)}, u32[]{:S(2)}, u32[]{:S(2)}) async-start(bf16[16,256,128]{2,1,0:T(8,128)(2,1)} %get-tuple-element.17), calls=%async_computation.2 | async-start | bytes 2097152 | tf_op jit(solution)/shard_map/all_to_all | solution.py:397
  83.8 0.0 copy-done.1
  83.8 0.0 copy-start
  83.8 1.0 convert_element_type.10
  84.8 14.0 %all-to-all-done.2 = bf16[16,256,128]{2,1,0:T(8,128)(2,1)S(1)} async-done(((bf16[16,256,128]{2,1,0:T(8,128)(2,1)}), bf16[16,256,128]{2,1,0:T(8,128)(2,1)S(1)}, u32[]{:S(2)}, u32[]{:S(2)}) %all-to-all-start.2) | async-done | bytes 1048608 | tf_op jit(solution)/shard_map/all_to_all | solution.py:397
  98.8 4.3 %all-to-all-start.4 = ((f16[16,32,896]{2,1,0:T(8,128)(2,1)}), f16[16,32,896]{2,1,0:T(8,128)(2,1)}, u32[]{:S(2)}, u32[]{:S(2)}) async-start(f16[16,32,896]{2,1,0:T(8,128)(2,1)} %convert_element_type.10), calls=%async_computation.4 | async-start | bytes 1835008 | tf_op jit(solution)/shard_map/all_to_all | solution.py:397
  103.1 0.0 copy-done
  103.2 1.8 %place_tiles.1.update_ref = bf16[16,32,896]{2,1,0:T(8,128)(2,1)} custom-call(s32[128]{0:T(128)S(1)} %copy-done, bf16[128,32,128]{2,1,0:T(8,128)(2,1)S(1)} %bitcast.3), custom_call_target="tpu_custom_call" | custom-call | tf_op jit(solution)/shard_map/place_tiles/pallas_call | solution.py:362
  105.0 12.2 %all-to-all-done.4 = f16[16,32,896]{2,1,0:T(8,128)(2,1)} async-done(((f16[16,32,896]{2,1,0:T(8,128)(2,1)}), f16[16,32,896]{2,1,0:T(8,128)(2,1)}, u32[]{:S(2)}, u32[]{:S(2)}) %all-to-all-start.4) | async-done | bytes 917536 | tf_op jit(solution)/shard_map/all_to_all | solution.py:397
  117.1 3.6 %all-to-all-start.3 = ((bf16[16,32,896]{2,1,0:T(8,128)(2,1)}), bf16[16,32,896]{2,1,0:T(8,128)(2,1)S(1)}, u32[]{:S(2)}, u32[]{:S(2)}) async-start(bf16[16,32,896]{2,1,0:T(8,128)(2,1)} %place_tiles.1.update_ref), calls=%async_computation.3 | async-start | bytes 1835008 | tf_op jit(solution)/shard_map/all_to_all | solution.py:397
  120.8 2.6 %convert_element_type.11.fast_ref = f32[16,32,896]{2,1,0:T(8,128)} convert(f16[16,32,896]{2,1,0:T(8,128)(2,1)} %all-to-all-done.4) | non-fusion elementwise | flops 458752 | bytes 2752512 | tf_op jit(solution)/shard_map/convert_element_type | solution.py:444
  123.4 6.6 %statistics.1 = (f32[2,512,512]{2,1,0:T(8,128)}, f32[2,512,512]{2,1,0:T(8,128)}, f32[2,512,512]{2,1,0:T(8,128)}) custom-call(s32[128]{0:T(128)} %tables.1.tab, f32[8,128]{1,0:T(8,128)} %get-tuple-element.18.scale_ref, bf16[2,512,512]{2,1,0:T(8,128)(2,1)} %get-tuple-element.19.grad_ref, f32[2,512,512]{2,1,0:T(8,128)} %left_ref.5, f32[2,512,512]{2,1,0:T(8,128)} %right_ref.5, ...), custom_call_target="tpu_custom_call" | custom-call | tf_op jit(solution)/shard_map/statistics/pallas_call | solution.py:336
  130.0 4.2 %pull_slow.1 = f32[32,14336]{1,0:T(8,128)} custom-call(f32[32,14336]{1,0:T(8,128)} %slow_ref.1, f32[16,32,896]{2,1,0:T(8,128)} %convert_element_type.11.fast_ref, bf16[16,32,896]{2,1,0:T(8,128)(2,1)} %place_tiles.1.update_ref), custom_call_target="tpu_custom_call" | custom-call | tf_op jit(solution)/shard_map/pull_slow/pallas_call | solution.py:385
  134.2 0.9 all-to-all-done.3
  135.2 1.5 %multiply_subtract_fusion = f32[16,32,896]{2,1,0:T(8,128)} fusion(f32[16,32,896]{2,1,0:T(8,128)S(1)} %bitcast.5, bf16[16,32,896]{2,1,0:T(8,128)(2,1)S(1)} %all-to-all-done.3), kind=kLoop, calls=%fused_computation | loop fusion | flops 1376256 | bytes 4587520 | tf_op jit(solution)/shard_map/sub | solution.py:445
Async XLA Ops:
  19.2 24.5 %all-to-all-start.1 = ((bf16[16,224,128]{2,1,0:T(8,128)(2,1)}), bf16[16,224,128]{2,1,0:T(8,128)(2,1)S(1)}, u32[]{:S(2)}, u32[]{:S(2)}) async-start(bf16[16,224,128]{2,1,0:T(8,128)(2,1)} %pack.3), calls=%async_computation.1 | async-start | bytes 1835008 | tf_op jit(solution)/shard_map/all_to_all | solution.py:397
  43.6 12.3 %copy-start.3 = (bf16[16,224,128]{2,1,0:T(8,128)(2,1)}, bf16[16,224,128]{2,1,0:T(8,128)(2,1)S(1)}, u32[]{:S(2)}) copy-start(bf16[16,224,128]{2,1,0:T(8,128)(2,1)S(1)} %all-to-all-done.1.rest_ref) | copy-start | bytes 2752516
  43.6 22.8 %all-to-all-start = ((bf16[16,320,128]{2,1,0:T(8,128)(2,1)}), bf16[16,320,128]{2,1,0:T(8,128)(2,1)S(1)}, u32[]{:S(2)}, u32[]{:S(2)}) async-start(bf16[16,320,128]{2,1,0:T(8,128)(2,1)} %pack.2), calls=%async_computation | async-start | bytes 2621440 | tf_op jit(solution)/shard_map/all_to_all | solution.py:397
  66.5 1.1 copy-start.2
  80.0 3.8 %copy-start.1 = (f32[512,896]{1,0:T(8,128)S(1)}, f32[512,896]{1,0:T(8,128)}, u32[]{:S(2)}) copy-start(f32[512,896]{1,0:T(8,128)} %param.14) | copy-start | bytes 5505028
  80.0 18.9 %all-to-all-start.2 = ((bf16[16,256,128]{2,1,0:T(8,128)(2,1)}), bf16[16,256,128]{2,1,0:T(8,128)(2,1)S(1)}, u32[]{:S(2)}, u32[]{:S(2)}) async-start(bf16[16,256,128]{2,1,0:T(8,128)(2,1)} %get-tuple-element.17), calls=%async_computation.2 | async-start | bytes 2097152 | tf_op jit(solution)/shard_map/all_to_all | solution.py:397
  83.8 19.4 %copy-start = (s32[128]{0:T(128)S(1)}, s32[128]{0:T(128)}, u32[]{:S(2)}) copy-start(s32[128]{0:T(128)} %tables.1.tab) | copy-start | bytes 1540
  98.8 18.3 %all-to-all-start.4 = ((f16[16,32,896]{2,1,0:T(8,128)(2,1)}), f16[16,32,896]{2,1,0:T(8,128)(2,1)}, u32[]{:S(2)}, u32[]{:S(2)}) async-start(f16[16,32,896]{2,1,0:T(8,128)(2,1)} %convert_element_type.10), calls=%async_computation.4 | async-start | bytes 1835008 | tf_op jit(solution)/shard_map/all_to_all | solution.py:397
  117.1 18.0 %all-to-all-start.3 = ((bf16[16,32,896]{2,1,0:T(8,128)(2,1)}), bf16[16,32,896]{2,1,0:T(8,128)(2,1)S(1)}, u32[]{:S(2)}, u32[]{:S(2)}) async-start(bf16[16,32,896]{2,1,0:T(8,128)(2,1)} %place_tiles.1.update_ref), calls=%async_computation.3 | async-start | bytes 1835008 | tf_op jit(solution)/shard_map/all_to_all | solution.py:397

commit v3 on v2

--- a/solution.py
+++ b/solution.py
@@ -1,5 +1,3 @@
-import functools
-
 import jax
 import jax.numpy as jnp
 from jax import lax
@@ -24,7 +22,6 @@
 F32 = jnp.float32
 BF16 = jnp.bfloat16
 TILE = 128
-SPLIT = 320
 MIB = 1 << 20
 
 
@@ -37,6 +34,7 @@
     return high, (x - high.astype(F32)).astype(BF16)
 
 
+WHOLE = pltpu.CompilerParams(vmem_limit_bytes=127 * MIB // 2)
 SMALL = pltpu.CompilerParams(vmem_limit_bytes=8 * MIB)
 PARAMS = pltpu.CompilerParams(vmem_limit_bytes=58 * MIB)
 
@@ -46,68 +44,92 @@
 HBM = pl.BlockSpec(memory_space=pltpu.HBM)
 
 
-def pack_tiles(gradient, tile_block, block_owner, peers, start, rows, parts=None):
-    cols = gradient.shape[1]
+def cut_tiles(gradient):
+    peers, rows, cols = gradient.shape
     tiles = cols // TILE
-    extra = 0 if parts is None else 32
-
-    def body(tb, owner, grad, *refs):
-        if extra:
-            parts_ref, out, tile_v, addends, in_sems, out_sems = refs
-        else:
-            out, tile_v, in_sems, out_sems = refs
-        row = lax.axis_index(DP)
-        column = lax.axis_index(TENSOR)
+    height = tiles * rows
+
+    def body(grad, out, tile_v, in_sems, out_sems):
         loads = []
         for i in range(tiles):
+            part = pl.ds(i * rows, rows)
             loads.append(
                 pltpu.make_async_copy(
-                    grad.at[pl.ds(start, rows), pl.ds(i * TILE, TILE)], tile_v.at[i], in_sems.at[i]
+                    grad.at[:, :, pl.ds(i * TILE, TILE)], tile_v.at[:, part], in_sems.at[i]
                 )
             )
             loads[-1].start()
         stores = []
 
-        def store(source, target, n):
-            stores.append(pltpu.make_async_copy(source, target, out_sems.at[n]))
+        def store(start, size, n):
+            part = pl.ds(start, size)
+            stores.append(
+                pltpu.make_async_copy(tile_v.at[:, part], out.at[:, part], out_sems.at[n])
+            )
             stores[-1].start()
 
-        if extra:
-            rest = parts_ref[...]
-            pieces = []
-            for _ in range(3):
-                piece = rest.astype(BF16).astype(F32)
-                pieces.append(piece)
-                rest = rest - piece
-            pieces.append(jnp.zeros_like(rest))
-            addends[...] = jnp.concatenate(pieces, axis=0).astype(BF16)
-            for p in range(peers):
-                store(addends, out.at[p, pl.ds(rows, extra)], tiles + p)
+        total = jnp.zeros((8, TILE), F32)
         for i in range(tiles):
-            slot = owner[tb[row, column * tiles + i]]
-            target = (slot >> 1) & (peers - 1)
             loads[i].wait()
-            store(tile_v.at[i], out.at[target, pl.ds(0, rows)], i)
+            store(i * rows, rows, i)
+            wide = tile_v[:, i * rows : (i + 1) * rows].astype(F32)
+            total = total + jnp.sum((wide * wide).reshape(-1, 8, TILE), axis=0)
+        rest = jnp.sum(total, axis=0, keepdims=True)
+        line = lax.broadcasted_iota(jnp.int32, (8, TILE), 0)
+        lines = jnp.zeros((8, TILE), F32)
+        for n in range(3):
+            piece = rest.astype(BF16).astype(F32)
+            lines = jnp.where(line == n, piece, lines)
+            rest = rest - piece
+        tile_v[:, height:] = jnp.broadcast_to(lines.astype(BF16)[None], (peers, 8, TILE))
+        store(height, 8, tiles)
         for copy in stores:
             copy.wait()
 
     return pl.pallas_call(
         body,
-        out_shape=jax.ShapeDtypeStruct((peers, rows + extra, TILE), BF16),
-        in_specs=[SMEM, SMEM, HBM] + ([VMEM] if extra else []),
+        out_shape=jax.ShapeDtypeStruct((peers, height + 8, TILE), BF16),
+        in_specs=[HBM],
         out_specs=HBM,
-        scratch_shapes=[pltpu.VMEM((tiles, rows, TILE), BF16)]
-        + ([pltpu.VMEM((extra, TILE), BF16)] if extra else [])
-        + [
+        scratch_shapes=[
+            pltpu.VMEM((peers, height + 8, TILE), BF16),
             pltpu.SemaphoreType.DMA((tiles,)),
-            pltpu.SemaphoreType.DMA((tiles + (peers if extra else 0),)),
+            pltpu.SemaphoreType.DMA((tiles + 1,)),
         ],
         compiler_params=PARAMS,
-        name="pack",
-    )(tile_block, block_owner, gradient, *([parts] if extra else []))
-
-
-def route_tables(tile_block, block_owner, tensor_size, shard_tiles, row_blocks, per_block):
+        name="cut_tiles",
+    )(gradient)
+
+
+def gather_tiles(tables, cut, places, rows):
+    peers, height, _ = cut.shape
+    height -= 8
+    tiles = height // rows
+
+    def body(tab, cut_ref, out, parts_out):
+        parts_out[...] = jnp.sum(cut_ref[:, height:].astype(F32), axis=0)
+
+        def step(p, c):
+            for i in range(tiles):
+                out[tab[p * tiles + i]] = cut_ref[p, i * rows : (i + 1) * rows]
+            return c
+
+        lax.fori_loop(0, peers, step, 0)
+
+    return pl.pallas_call(
+        body,
+        out_shape=(
+            jax.ShapeDtypeStruct((places, rows, TILE), BF16),
+            jax.ShapeDtypeStruct((8, TILE), F32),
+        ),
+        in_specs=[SMEM, VMEM],
+        out_specs=(VMEM, VMEM),
+        compiler_params=SMALL,
+        name="gather_tiles",
+    )(tables, cut)
+
+
+def route_tables(tile_block, block_owner, tensor_size, row_blocks, per_block):
     tile_count = tile_block.shape[1]
 
     def body(tb, owner, out, count):
@@ -119,7 +141,7 @@
             return c
 
         lax.fori_loop(0, row_blocks, clear, 0)
-        for i in range(tile_count, tile_count + 16):
+        for i in range(tile_count, 128):
             out[i] = 0
 
         def step(g, c):
@@ -132,8 +154,7 @@
 
             @pl.when((slot >> 1) == mine)
             def _():
-                out[tile_count + (slot & 1) * per_block + j] = g // shard_tiles
-                out[tile_count + 8 + (slot & 1)] = 1
+                out[tile_count + (slot & 1)] = 1
 
             return c
 
@@ -145,32 +166,13 @@
         in_specs=[SMEM, SMEM],
         out_specs=SMEM,
         scratch_shapes=[pltpu.SMEM((row_blocks,), jnp.int32)],
-        compiler_params=PARAMS,
+        compiler_params=SMALL,
         name="tables",
     )(tile_block, block_owner)
 
 
-def square_parts(gradient):
-    def body(grad, out):
-        wide = grad[...].astype(F32)
-        rows, cols = wide.shape
-        part = jnp.sum((wide * wide).reshape(rows // 8, 8, cols), axis=0)
-        out[...] = functools.reduce(
-            jnp.add, [part[:, c : c + TILE] for c in range(0, cols, TILE)]
-        )
-
-    return pl.pallas_call(
-        body,
-        out_shape=jax.ShapeDtypeStruct((8, TILE), F32),
-        in_specs=[VMEM],
-        out_specs=VMEM,
-        compiler_params=PARAMS,
-        name="square_parts",
-    )(gradient)
-
-
 def clip_factor(parts, total_count):
-    total = jnp.sum(jnp.sum(parts.astype(F32), axis=0), keepdims=True)
+    total = jnp.sum(parts, keepdims=True)
     return CLIP_RMS / jnp.sqrt(total / total_count + 1e-06)
 
 
@@ -203,31 +205,24 @@
     )(left, right, moment)
 
 
-def main_step(tables, first, rest, turned, left_t, left, right, second, base, total_count):
+def main_step(tables, parts, other, arrived, turned, left_t, left, right, second, base, total_count):
     slots, size, _ = left.shape
     per_block = size // TILE
-    peers, split, _ = first.shape
+    peers = arrived.shape[0]
     rows = size // peers
-    names = 5 + 2 * per_block
+    names = 5 + per_block
 
     def body(
-        tab, first_ref, rest_ref, turned_ref, left_t_ref, left_ref, right_ref, second_ref,
+        tab, parts_ref, other_ref, arrived_ref, turned_ref, left_t_ref, left_ref, right_ref, second_ref,
         second_out, send_out, grad_out, scale_out,
-        grad_v, left_t_v, right_v, second_v, turned_v, left_v, new_v, send_v, parts_v, sems,
-        out_sems,
+        grad_v, left_t_v, right_v, second_v, turned_v, left_v, new_v, send_v, sems, out_sems,
     ):
         def loads(k):
             pairs = [(left_t_ref.at[k], left_t_v.at[k])]
             for j in range(per_block):
-                source = tab[base + k * per_block + j]
+                place = pl.ds((k * per_block + j) * rows, rows)
                 cols = pl.ds(j * TILE, TILE)
-                pairs.append((first_ref.at[source], grad_v.at[k, pl.ds(0, split), cols]))
-                pairs.append(
-                    (
-                        rest_ref.at[source, pl.ds(0, size - split)],
-                        grad_v.at[k, pl.ds(split, size - split), cols],
-                    )
-                )
+                pairs.append((arrived_ref.at[:, place], grad_v.at[k, :, :, cols]))
             pairs += [
                 (right_ref.at[k], right_v.at[k]),
                 (second_ref.at[k], second_v.at[k]),
@@ -239,15 +234,9 @@
             ]
 
         copies = [loads(k) for k in range(slots)]
-        parts_copy = pltpu.make_async_copy(
-            rest_ref.at[:, pl.ds(size - split, 32)], parts_v, out_sems.at[0, 3]
-        )
-        parts_copy.start()
-        for group in copies:
-            for copy in group:
-                copy.start()
-        parts_copy.wait()
-        scale = clip_factor(parts_v[...], total_count)
+        for copy in copies[0]:
+            copy.start()
+        scale = clip_factor(parts_ref[...] + other_ref[...], total_count)
         scale_out[...] = jnp.broadcast_to(scale, scale_out.shape)
         outs = []
 
@@ -260,14 +249,17 @@
             for copy in wait[:-4]:
                 copy.wait()
             emit(grad_v.at[k], grad_out.at[k], k, 2)
-            high, low = halves(dot(left_t_v[k], grad_v[k]))
+            if k + 1 < slots:
+                for copy in copies[k + 1]:
+                    copy.start()
+            high, low = halves(dot(left_t_v[k], grad_v[k].reshape(size, size)))
             wait[-4].wait()
             right_wide = right_v[k]
             rotated = scale * (dot(high, right_wide) + dot(low, right_wide))
             wait[-3].wait()
             old = second_v[k]
             new = BETA_TWO * old + (1.0 - BETA_TWO) * rotated * rotated
-            new_v[k] = jnp.where(tab[base + 8 + k] == 1, new, old)
+            new_v[k] = jnp.where(tab[base + k] == 1, new, old)
             emit(new_v.at[k], second_out.at[k], k, 0)
             wait[-2].wait()
             direction = (BETA_ONE * turned_v[k] + (1.0 - BETA_ONE) * rotated) / (
@@ -295,23 +287,23 @@
         out_shape=(
             jax.ShapeDtypeStruct(square, F32),
             jax.ShapeDtypeStruct((peers, slots * per_block * rows, TILE), BF16),
-            jax.ShapeDtypeStruct(square, BF16),
+            jax.ShapeDtypeStruct((slots, peers, rows, size), BF16),
             jax.ShapeDtypeStruct((8, TILE), F32),
         ),
-        in_specs=[SMEM] + [HBM] * 7,
+        in_specs=[SMEM, VMEM, VMEM] + [HBM] * 6,
         out_specs=(HBM, HBM, HBM, VMEM),
-        scratch_shapes=[pltpu.VMEM(square, BF16)] * 3
+        scratch_shapes=[pltpu.VMEM((slots, peers, rows, size), BF16)]
+        + [pltpu.VMEM(square, BF16)] * 2
         + [pltpu.VMEM(square, F32)] * 2
         + [pltpu.VMEM(square, BF16), pltpu.VMEM(square, F32)]
         + [
             pltpu.VMEM((peers, slots * per_block * rows, TILE), BF16),
-            pltpu.VMEM((peers, 32, TILE), BF16),
             pltpu.SemaphoreType.DMA((slots, names)),
-            pltpu.SemaphoreType.DMA((slots, 4)),
+            pltpu.SemaphoreType.DMA((slots, 3)),
         ],
-        compiler_params=PARAMS,
+        compiler_params=WHOLE,
         name="main_step",
-    )(tables, first, rest, turned, left_t, left, right, second)
+    )(tables, parts, other, arrived, turned, left_t, left, right, second)
 
 
 def statistics(tables, scale, grad, left_stat, right_stat, moment, base):
@@ -319,7 +311,7 @@
 
     def body(tab, scale_ref, grad_ref, left_ref, right_ref, moment_ref, *outs):
         left_out, right_out, moment_out = outs
-        here = tab[base + 8 + pl.program_id(0)] == 1
+        here = tab[base + pl.program_id(0)] == 1
         scale = scale_ref[0:1, 0:1]
         squared = (1.0 - BETA_STAT) * (scale * scale)
         grad = grad_ref[0]
@@ -419,29 +411,33 @@
     row_blocks = block_owner.shape[0] // row_groups
     total_count = row_count * shard_cols * lax.axis_size(DP) * peers
 
-    first = pack_tiles(gradient, tile_block, block_owner, peers, 0, SPLIT)
-    first = exchange(first)
-    parts = square_parts(gradient)
-    parts = functools.reduce(lax.psum, DP, parts)
-    rest = pack_tiles(gradient, tile_block, block_owner, peers, SPLIT, size - SPLIT, parts)
-    rest = exchange(rest)
-    tables = route_tables(tile_block, block_owner, peers, shard_tiles, row_blocks, per_block)
+    rows = row_count // peers
+    places = peers * slots * per_block
+    cut = exchange(cut_tiles(gradient.reshape(peers, rows, shard_cols)))
+    tables = route_tables(tile_block, block_owner, peers, row_blocks, per_block)
+    outgoing, parts = gather_tiles(tables, cut, places, rows)
+    arrived = exchange(outgoing.reshape(peers, slots * per_block * rows, TILE))
+    parts = lax.psum(parts, DP[0])
+    pairs = [(i, i ^ 1) for i in range(lax.axis_size(DP[1]))]
+    other = lax.ppermute(parts, DP[1], pairs)
     turned, left_t = turn_moment(left_basis, right_basis, first_moment)
-    by_rows = (peers, row_count // peers, shard_cols)
+    by_rows = (peers, rows, shard_cols)
     fast_half = fast_weight.reshape(by_rows).astype(jnp.float16)
     fast_rows = exchange(fast_half)
     second_new, send, grad, scale = main_step(
-        tables, first, rest, turned, left_t, left_basis, right_basis, second_moment,
+        tables, parts, other, arrived, turned, left_t, left_basis, right_basis, second_moment,
         tile_count, total_count,
     )
     received = exchange(send)
+    fast_rows, grad = lax.optimization_barrier((fast_rows.astype(F32), grad))
     left_new, right_new, moment_new = statistics(
-        tables, scale, grad, left_stat, right_stat, first_moment, tile_count
+        tables, scale, grad.reshape(slots, size, size), left_stat, right_stat, first_moment,
+        tile_count,
     )
-    received = received.reshape(peers * slots * per_block, row_count // peers, TILE)
+    received = received.reshape(places, rows, TILE)
     update_rows = place_tiles(tables, received, shard_tiles)
     home = exchange(update_rows)
-    slow_new = pull_slow(slow_flat, fast_rows.astype(F32), update_rows)
+    slow_new = pull_slow(slow_flat, fast_rows, update_rows)
     fast_new = fast_weight.reshape(by_rows) - STEP_RATE * home.astype(F32)
     fast_new = fast_new.reshape(row_count, shard_cols)
     return (fast_new, slow_new, left_new, right_new, moment_new, second_new)

time: 138 us -> 125 us (0.906)
  waiting for transfers between devices: 51.5 us -> 44.3 us
  Pallas kernels: 40.8 us -> 35 us
  starting transfers between devices: 23.3 us -> 27.6 us
  blocking collectives: 14 us -> 10.8 us
    all_to_all x5, waiting for transfers between devices: 51.5 us -> 44.3 us  [exchange(): return lax.all_to_all(x, axes, split_axis=0, concat_axis=0, tiled=True)]
    all_to_all x5, starting transfers between devices: 23.3 us -> 27.5 us  [exchange(): return lax.all_to_all(x, axes, split_axis=0, concat_axis=0, tiled=True)]
    pallas_call x3 -> x2, Pallas kernels: 7.19 us -> 3.89 us  [the longest x1 2.18 us: cut_tiles(): pl.pallas_call(body, out_shape=jax.ShapeDtypeStruct((peers, height + 8, T...]
    psum x2 -> x1, blocking collectives: 14 us -> 10.8 us  [on_device(): parts = lax.psum(parts, DP[0])]
    pallas_call x1, Pallas kernels: 12.4 us -> 10.2 us  [main_step(): pl.pallas_call(body, out_shape=(jax.ShapeDtypeStruct(square, F32), jax.Sh...]
  transfers between devices with their start and end apart: 5 -> 6, of which waited for: 5 -> 4; matrix products, arithmetic and copies ran while one was open for 3% -> 3% of each run, Pallas kernels for 17% -> 17%
where the time goes in v3:
time: 125 us; the launch traced here: 124 us
  waiting for transfers between devices  44.3 us (35%)
  Pallas kernels  35 us (28%)
  starting transfers between devices  27.6 us (22%)
  blocking collectives  10.8 us (9%)
  other arithmetic  5.15 us (4%)
    all_to_all x5, waiting for transfers between devices, exchange(): return lax.all_to_all(x, axes, split_axis=0, concat_axis=0, tiled=True)  44.3 us
    all_to_all x5, starting transfers between devices, exchange(): return lax.all_to_all(x, axes, split_axis=0, concat_axis=0, tiled=True)  27.5 us
    psum x1, blocking collectives, on_device(): parts = lax.psum(parts, DP[0])  10.8 us
    pallas_call x1, Pallas kernels, main_step(): pl.pallas_call(body, out_shape=(jax.ShapeDtypeStruct(square, F32), jax.Sh...  10.2 us
    pallas_call x1, Pallas kernels, statistics(): pl.pallas_call(body, grid_spec=pltpu.PrefetchScalarGridSpec(num_scalar_pr...  6.61 us
    pallas_call x1, Pallas kernels, turn_moment(): pl.pallas_call(body, grid=(slots,), out_shape=(jax.ShapeDtypeStruct((slot...  5.14 us
    pallas_call x1, Pallas kernels, pull_slow(): pl.pallas_call(body, grid=(peers // step,), out_shape=jax.ShapeDtypeStruc...  4.24 us
    pallas_call x1, Pallas kernels, route_tables(): pl.pallas_call(body, out_shape=jax.ShapeDtypeStruct((128,), jnp.int32), i...  3.11 us
  transfers between devices with their start and end apart: 6, of which 4 were waited for; matrix products, arithmetic and copies ran while one was open for 3% of the time, Pallas kernels for 17%

profile of v3, /device:TPU:0, one launch (start us, length us, event | category | flops | bytes accessed | tf_op | source)
XLA Modules:
  0.0 124.1 jit_solution(5353517814403335340)
XLA Ops:
  0.6 0.0 copy-start.2
  0.6 0.0 copy-start.3
  0.7 2.2 %cut_tiles.1 = bf16[16,232,128]{2,1,0:T(8,128)(2,1)} custom-call(bf16[16,32,896]{2,1,0:T(8,128)(2,1)} %bitcast.11), custom_call_target="tpu_custom_call" | custom-call | tf_op jit(solution)/shard_map/cut_tiles/pallas_call | solution.py:89
  2.8 8.0 %all-to-all-start = ((bf16[16,232,128]{2,1,0:T(8,128)(2,1)}), bf16[16,232,128]{2,1,0:T(8,128)(2,1)S(1)}, u32[]{:S(2)}, u32[]{:S(2)}) async-start(bf16[16,232,128]{2,1,0:T(8,128)(2,1)} %cut_tiles.1), calls=%async_computation | async-start | bytes 1900544 | tf_op jit(solution)/shard_map/all_to_all | solution.py:389
  10.8 0.0 copy-done.2
  10.9 0.0 copy-done.3
  10.9 3.1 %tables.1.tab = s32[128]{0:T(128)S(1)} custom-call(s32[8,112]{1,0:T(8,128)S(1)} %copy-done.2, s32[224]{0:T(256)S(1)} %copy-done.3), custom_call_target="tpu_custom_call" | custom-call | tf_op jit(solution)/shard_map/tables/pallas_call | solution.py:163
  14.0 0.0 copy-start
  14.0 13.4 %all-to-all-done.cut_ref = bf16[16,232,128]{2,1,0:T(8,128)(2,1)S(1)} async-done(((bf16[16,232,128]{2,1,0:T(8,128)(2,1)}), bf16[16,232,128]{2,1,0:T(8,128)(2,1)S(1)}, u32[]{:S(2)}, u32[]{:S(2)}) %all-to-all-start) | async-done | bytes 950304 | tf_op jit(solution)/shard_map/all_to_all | solution.py:389
  27.4 1.7 %gather_tiles.1 = (bf16[128,32,128]{2,1,0:T(8,128)(2,1)}, f32[8,128]{1,0:T(8,128)S(1)}) custom-call(s32[128]{0:T(128)S(1)} %tables.1.tab, bf16[16,232,128]{2,1,0:T(8,128)(2,1)S(1)} %all-to-all-done.cut_ref), custom_call_target="tpu_custom_call" | custom-call | tf_op jit(solution)/shard_map/gather_tiles/pallas_call | solution.py:119
  29.1 4.3 %all-to-all-start.1 = ((bf16[16,256,128]{2,1,0:T(8,128)(2,1)}), bf16[16,256,128]{2,1,0:T(8,128)(2,1)}, u32[]{:S(2)}, u32[]{:S(2)}) async-start(bf16[16,256,128]{2,1,0:T(8,128)(2,1)} %bitcast.2), calls=%async_computation.1 | async-start | bytes 2097152 | tf_op jit(solution)/shard_map/all_to_all | solution.py:389
  33.4 10.8 %psum.7.parts_ref = f32[8,128]{1,0:T(8,128)S(1)} all-reduce(f32[8,128]{1,0:T(8,128)S(1)} %get-tuple-element.19), channel_id=1, replica_groups=mesh['dp_0'=4,'dp_1'=2,'tensor_0'=4,'tensor_1'=4] {'dp_0'}, use_global_device_ids=true, to_apply=%region_0.0 | all-reduce | flops 1024 | bytes 8192 | tf_op jit(solution)/shard_map/psum | solution.py:420
  44.2 0.0 copy-start.5
  44.2 0.1 collective-permute-start
  44.3 5.1 %turn_moment.1 = (f32[2,512,512]{2,1,0:T(8,128)}, bf16[2,512,512]{2,1,0:T(8,128)(2,1)}) custom-call(bf16[2,512,512]{2,1,0:T(8,128)(2,1)} %left_ref.4, bf16[2,512,512]{2,1,0:T(8,128)(2,1)} %right_ref.4, f32[2,512,512]{2,1,0:T(8,128)} %moment_ref.3), custom_call_target="tpu_custom_call" | custom-call | tf_op jit(solution)/shard_map/turn_moment/pallas_call | solution.py:194
  49.4 0.0 copy-done
  49.4 0.0 copy-done.5
  49.4 0.0 collective-permute-done.other_ref
  49.4 0.0 copy-start.6
  49.4 0.0 all-to-all-done.1.arrived_ref
  49.4 0.6 copy-done.6
  50.0 10.2 %main_step.1 = (f32[2,512,512]{2,1,0:T(8,128)}, bf16[16,256,128]{2,1,0:T(8,128)(2,1)}, bf16[2,16,32,512]{3,2,1,0:T(8,128)(2,1)}, f32[8,128]{1,0:T(8,128)}) custom-call(s32[128]{0:T(128)} %copy-done, f32[8,128]{1,0:T(8,128)} %copy-done.5, f32[8,128]{1,0:T(8,128)} %copy-done.6, bf16[16,256,128]{2,1,0:T(8,128)(2,1)} %all-to-all-done.1.arrived_ref, ...), custom_call_target="tpu_custom_call" | custom-call | tf_op jit(solution)/shard_map/main_step/pallas_call | solution.py:285
  60.2 0.0 copy-start.4
  60.2 7.2 %all-to-all-start.2 = ((bf16[16,256,128]{2,1,0:T(8,128)(2,1)}), bf16[16,256,128]{2,1,0:T(8,128)(2,1)S(1)}, u32[]{:S(2)}, u32[]{:S(2)}) async-start(bf16[16,256,128]{2,1,0:T(8,128)(2,1)} %get-tuple-element.23), calls=%async_computation.2 | async-start | bytes 2097152 | tf_op jit(solution)/shard_map/all_to_all | solution.py:389
  67.4 0.0 copy-done.4
  67.4 0.0 copy-start.1
  67.5 1.0 convert_element_type.10
  68.5 17.4 %all-to-all-done.2 = bf16[16,256,128]{2,1,0:T(8,128)(2,1)S(1)} async-done(((bf16[16,256,128]{2,1,0:T(8,128)(2,1)}), bf16[16,256,128]{2,1,0:T(8,128)(2,1)S(1)}, u32[]{:S(2)}, u32[]{:S(2)}) %all-to-all-start.2) | async-done | bytes 1048608 | tf_op jit(solution)/shard_map/all_to_all | solution.py:389
  85.9 4.3 %all-to-all-start.4 = ((f16[16,32,896]{2,1,0:T(8,128)(2,1)}), f16[16,32,896]{2,1,0:T(8,128)(2,1)}, u32[]{:S(2)}, u32[]{:S(2)}) async-start(f16[16,32,896]{2,1,0:T(8,128)(2,1)} %convert_element_type.10), calls=%async_computation.4 | async-start | bytes 1835008 | tf_op jit(solution)/shard_map/all_to_all | solution.py:389
  90.2 0.0 copy-done.1
  90.2 1.8 %place_tiles.1.update_ref = bf16[16,32,896]{2,1,0:T(8,128)(2,1)} custom-call(s32[128]{0:T(128)S(1)} %copy-done.1, bf16[128,32,128]{2,1,0:T(8,128)(2,1)S(1)} %bitcast.6), custom_call_target="tpu_custom_call" | custom-call | tf_op jit(solution)/shard_map/place_tiles/pallas_call | solution.py:354
  92.0 12.7 %all-to-all-done.4 = f16[16,32,896]{2,1,0:T(8,128)(2,1)} async-done(((f16[16,32,896]{2,1,0:T(8,128)(2,1)}), f16[16,32,896]{2,1,0:T(8,128)(2,1)}, u32[]{:S(2)}, u32[]{:S(2)}) %all-to-all-start.4) | async-done | bytes 917536 | tf_op jit(solution)/shard_map/all_to_all | solution.py:389
  104.8 3.6 %all-to-all-start.3 = ((bf16[16,32,896]{2,1,0:T(8,128)(2,1)}), bf16[16,32,896]{2,1,0:T(8,128)(2,1)S(1)}, u32[]{:S(2)}, u32[]{:S(2)}) async-start(bf16[16,32,896]{2,1,0:T(8,128)(2,1)} %place_tiles.1.update_ref), calls=%async_computation.3 | async-start | bytes 1835008 | tf_op jit(solution)/shard_map/all_to_all | solution.py:389
  108.4 2.6 %convert_element_type.11.fast_ref = f32[16,32,896]{2,1,0:T(8,128)} convert(f16[16,32,896]{2,1,0:T(8,128)(2,1)} %all-to-all-done.4) | non-fusion elementwise | flops 458752 | bytes 2752512 | tf_op jit(solution)/shard_map/convert_element_type | solution.py:432
  111.0 6.6 %statistics.1 = (f32[2,512,512]{2,1,0:T(8,128)}, f32[2,512,512]{2,1,0:T(8,128)}, f32[2,512,512]{2,1,0:T(8,128)}) custom-call(s32[128]{0:T(128)} %copy-done, f32[8,128]{1,0:T(8,128)} %get-tuple-element.26.scale_ref, bf16[2,512,512]{2,1,0:T(8,128)(2,1)} %bitcast.10, f32[2,512,512]{2,1,0:T(8,128)} %left_ref.5, f32[2,512,512]{2,1,0:T(8,128)} %right_ref.5, ...), custom_call_target="tpu_custom_call" | custom-call | tf_op jit(solution)/shard_map/statistics/pallas_call | solution.py:328
  117.6 4.2 %pull_slow.1 = f32[32,14336]{1,0:T(8,128)} custom-call(f32[32,14336]{1,0:T(8,128)} %slow_ref.1, f32[16,32,896]{2,1,0:T(8,128)} %convert_element_type.11.fast_ref, bf16[16,32,896]{2,1,0:T(8,128)(2,1)} %place_tiles.1.update_ref), custom_call_target="tpu_custom_call" | custom-call | tf_op jit(solution)/shard_map/pull_slow/pallas_call | solution.py:377
  121.9 0.8 all-to-all-done.3
  122.6 1.5 %multiply_subtract_fusion = f32[16,32,896]{2,1,0:T(8,128)} fusion(f32[16,32,896]{2,1,0:T(8,128)S(1)} %bitcast.8, bf16[16,32,896]{2,1,0:T(8,128)(2,1)S(1)} %all-to-all-done.3), kind=kLoop, calls=%fused_computation | loop fusion | flops 1376256 | bytes 4587520 | tf_op jit(solution)/shard_map/sub | solution.py:441
Async XLA Ops:
  0.6 10.2 %copy-start.2 = (s32[8,112]{1,0:T(8,128)S(1)}, s32[8,112]{1,0:T(8,128)}, u32[]{:S(2)}) copy-start(s32[8,112]{1,0:T(8,128)} %tb.1) | copy-start | bytes 10756
  0.6 10.2 %copy-start.3 = (s32[224]{0:T(256)S(1)}, s32[224]{0:T(256)}, u32[]{:S(2)}) copy-start(s32[224]{0:T(256)} %owner.1) | copy-start | bytes 2692
  2.8 24.5 %all-to-all-start = ((bf16[16,232,128]{2,1,0:T(8,128)(2,1)}), bf16[16,232,128]{2,1,0:T(8,128)(2,1)S(1)}, u32[]{:S(2)}, u32[]{:S(2)}) async-start(bf16[16,232,128]{2,1,0:T(8,128)(2,1)} %cut_tiles.1), calls=%async_computation | async-start | bytes 1900544 | tf_op jit(solution)/shard_map/all_to_all | solution.py:389
  14.0 35.4 %copy-start = (s32[128]{0:T(128)}, s32[128]{0:T(128)S(1)}, u32[]{:S(2)}) copy-start(s32[128]{0:T(128)S(1)} %tables.1.tab) | copy-start | bytes 1540
  29.1 20.4 %all-to-all-start.1 = ((bf16[16,256,128]{2,1,0:T(8,128)(2,1)}), bf16[16,256,128]{2,1,0:T(8,128)(2,1)}, u32[]{:S(2)}, u32[]{:S(2)}) async-start(bf16[16,256,128]{2,1,0:T(8,128)(2,1)} %bitcast.2), calls=%async_computation.1 | async-start | bytes 2097152 | tf_op jit(solution)/shard_map/all_to_all | solution.py:389
  44.2 5.2 %copy-start.5 = (f32[8,128]{1,0:T(8,128)}, f32[8,128]{1,0:T(8,128)S(1)}, u32[]{:S(2)}) copy-start(f32[8,128]{1,0:T(8,128)S(1)} %psum.7.parts_ref) | copy-start | bytes 12292
  44.2 5.2 %collective-permute-start = (f32[8,128]{1,0:T(8,128)S(1)}, f32[8,128]{1,0:T(8,128)S(1)}, u32[]{:S(2)}, u32[]{:S(2)}) collective-permute-start(f32[8,128]{1,0:T(8,128)S(1)} %psum.7.parts_ref), channel_id=1, source_target_pairs={{0,16},{16,0},{1,17},{17,1},{2,18},{18,2},{3,19},{19,3},{4,20},{20... | collective-permute-start | bytes 12296 | tf_op jit(solution)/shard_map/ppermute | solution.py:422
  49.4 0.6 copy-start.6
  60.2 7.2 %copy-start.4 = (f32[512,896]{1,0:T(8,128)S(1)}, f32[512,896]{1,0:T(8,128)}, u32[]{:S(2)}) copy-start(f32[512,896]{1,0:T(8,128)} %param.14) | copy-start | bytes 5505028
  60.2 25.7 %all-to-all-start.2 = ((bf16[16,256,128]{2,1,0:T(8,128)(2,1)}), bf16[16,256,128]{2,1,0:T(8,128)(2,1)S(1)}, u32[]{:S(2)}, u32[]{:S(2)}) async-start(bf16[16,256,128]{2,1,0:T(8,128)(2,1)} %get-tuple-element.23), calls=%async_computation.2 | async-start | bytes 2097152 | tf_op jit(solution)/shard_map/all_to_all | solution.py:389
  67.4 22.8 %copy-start.1 = (s32[128]{0:T(128)S(1)}, s32[128]{0:T(128)}, u32[]{:S(2)}) copy-start(s32[128]{0:T(128)} %copy-done) | copy-start | bytes 1540
  85.9 18.9 %all-to-all-start.4 = ((f16[16,32,896]{2,1,0:T(8,128)(2,1)}), f16[16,32,896]{2,1,0:T(8,128)(2,1)}, u32[]{:S(2)}, u32[]{:S(2)}) async-start(f16[16,32,896]{2,1,0:T(8,128)(2,1)} %convert_element_type.10), calls=%async_computation.4 | async-start | bytes 1835008 | tf_op jit(solution)/shard_map/all_to_all | solution.py:389
  104.8 17.9 %all-to-all-start.3 = ((bf16[16,32,896]{2,1,0:T(8,128)(2,1)}), bf16[16,32,896]{2,1,0:T(8,128)(2,1)S(1)}, u32[]{:S(2)}, u32[]{:S(2)}) async-start(bf16[16,32,896]{2,1,0:T(8,128)(2,1)} %place_tiles.1.update_ref), calls=%async_computation.3 | async-start | bytes 1835008 | tf_op jit(solution)/shard_map/all_to_all | solution.py:389

commit v4 on v3

--- a/solution.py
+++ b/solution.py
@@ -109,12 +109,9 @@
     def body(tab, cut_ref, out, parts_out):
         parts_out[...] = jnp.sum(cut_ref[:, height:].astype(F32), axis=0)
 
-        def step(p, c):
+        for p in range(peers):
             for i in range(tiles):
                 out[tab[p * tiles + i]] = cut_ref[p, i * rows : (i + 1) * rows]
-            return c
-
-        lax.fori_loop(0, peers, step, 0)
 
     return pl.pallas_call(
         body,
@@ -342,20 +339,29 @@
 def place_tiles(tables, received, shard_tiles):
     places, rows, _ = received.shape
     peers = places // 8
-
-    def body(tab, received_ref, out):
-        def step(p, c):
-            for i in range(shard_tiles):
-                out[p, :, i * TILE : (i + 1) * TILE] = received_ref[tab[p * shard_tiles + i]]
-            return c
-
-        lax.fori_loop(0, peers, step, 0)
-
-    return pl.pallas_call(
-        body,
-        out_shape=jax.ShapeDtypeStruct((peers, rows, shard_tiles * TILE), BF16),
+    groups = 4
+    step = peers // groups
+    shape = (peers, rows, shard_tiles * TILE)
+
+    def body(tab, received_ref, out, out_v, sems):
+        copies = []
+        for n in range(groups):
+            for p in range(n * step, (n + 1) * step):
+                for i in range(shard_tiles):
+                    tile = received_ref[tab[p * shard_tiles + i]]
+                    out_v[p, :, i * TILE : (i + 1) * TILE] = tile
+            part = pl.ds(n * step, step)
+            copies.append(pltpu.make_async_copy(out_v.at[part], out.at[part], sems.at[n]))
+            copies[-1].start()
+        for copy in copies:
+            copy.wait()
+
+    return pl.pallas_call(
+        body,
+        out_shape=jax.ShapeDtypeStruct(shape, BF16),
         in_specs=[SMEM, VMEM],
-        out_specs=VMEM,
+        out_specs=HBM,
+        scratch_shapes=[pltpu.VMEM(shape, BF16), pltpu.SemaphoreType.DMA((groups,))],
         compiler_params=SMALL,
         name="place_tiles",
     )(tables, received)

time: 125 us -> 125 us (level)
  no operation moved by 1% of the time
where the time goes in v4:
time: 125 us; the launch traced here: 124 us
  waiting for transfers between devices  44.6 us (36%)
  Pallas kernels  34.6 us (28%)
  starting transfers between devices  27.6 us (22%)
  blocking collectives  10.8 us (9%)
  other arithmetic  5.15 us (4%)
    all_to_all x5, waiting for transfers between devices, exchange(): return lax.all_to_all(x, axes, split_axis=0, concat_axis=0, tiled=True)  44.6 us
    all_to_all x5, starting transfers between devices, exchange(): return lax.all_to_all(x, axes, split_axis=0, concat_axis=0, tiled=True)  27.5 us
    psum x1, blocking collectives, on_device(): parts = lax.psum(parts, DP[0])  10.8 us
    pallas_call x1, Pallas kernels, main_step(): pl.pallas_call(body, out_shape=(jax.ShapeDtypeStruct(square, F32), jax.Sh...  10.2 us
    pallas_call x1, Pallas kernels, statistics(): pl.pallas_call(body, grid_spec=pltpu.PrefetchScalarGridSpec(num_scalar_pr...  6.61 us
    pallas_call x1, Pallas kernels, turn_moment(): pl.pallas_call(body, grid=(slots,), out_shape=(jax.ShapeDtypeStruct((slot...  5.14 us
    pallas_call x1, Pallas kernels, pull_slow(): pl.pallas_call(body, grid=(peers // step,), out_shape=jax.ShapeDtypeStruc...  4.24 us
    pallas_call x1, Pallas kernels, route_tables(): pl.pallas_call(body, out_shape=jax.ShapeDtypeStruct((128,), jnp.int32), i...  3.11 us
  transfers between devices with their start and end apart: 6, of which 4 were waited for; matrix products, arithmetic and copies ran while one was open for 3% of the time, Pallas kernels for 17%

profile of v4, /device:TPU:0, one launch (start us, length us, event | category | flops | bytes accessed | tf_op | source)
XLA Modules:
  0.0 124.1 jit_solution(9898824997684757063)
XLA Ops:
  0.6 0.0 copy-start.2
  0.6 0.0 copy-start.3
  0.7 2.2 %cut_tiles.1 = bf16[16,232,128]{2,1,0:T(8,128)(2,1)} custom-call(bf16[16,32,896]{2,1,0:T(8,128)(2,1)} %bitcast.11), custom_call_target="tpu_custom_call" | custom-call | tf_op jit(solution)/shard_map/cut_tiles/pallas_call | solution.py:89
  2.8 8.0 %all-to-all-start = ((bf16[16,232,128]{2,1,0:T(8,128)(2,1)}), bf16[16,232,128]{2,1,0:T(8,128)(2,1)S(1)}, u32[]{:S(2)}, u32[]{:S(2)}) async-start(bf16[16,232,128]{2,1,0:T(8,128)(2,1)} %cut_tiles.1), calls=%async_computation | async-start | bytes 1900544 | tf_op jit(solution)/shard_map/all_to_all | solution.py:395
  10.8 0.0 copy-done.2
  10.9 0.0 copy-done.3
  10.9 3.1 %tables.1.tab = s32[128]{0:T(128)S(1)} custom-call(s32[8,112]{1,0:T(8,128)S(1)} %copy-done.2, s32[224]{0:T(256)S(1)} %copy-done.3), custom_call_target="tpu_custom_call" | custom-call | tf_op jit(solution)/shard_map/tables/pallas_call | solution.py:160
  14.0 0.0 copy-start
  14.0 13.4 %all-to-all-done.cut_ref = bf16[16,232,128]{2,1,0:T(8,128)(2,1)S(1)} async-done(((bf16[16,232,128]{2,1,0:T(8,128)(2,1)}), bf16[16,232,128]{2,1,0:T(8,128)(2,1)S(1)}, u32[]{:S(2)}, u32[]{:S(2)}) %all-to-all-start) | async-done | bytes 950304 | tf_op jit(solution)/shard_map/all_to_all | solution.py:395
  27.4 1.6 %gather_tiles.1 = (bf16[128,32,128]{2,1,0:T(8,128)(2,1)}, f32[8,128]{1,0:T(8,128)S(1)}) custom-call(s32[128]{0:T(128)S(1)} %tables.1.tab, bf16[16,232,128]{2,1,0:T(8,128)(2,1)S(1)} %all-to-all-done.cut_ref), custom_call_target="tpu_custom_call" | custom-call | tf_op jit(solution)/shard_map/gather_tiles/pallas_call | solution.py:116
  29.0 4.3 %all-to-all-start.1 = ((bf16[16,256,128]{2,1,0:T(8,128)(2,1)}), bf16[16,256,128]{2,1,0:T(8,128)(2,1)}, u32[]{:S(2)}, u32[]{:S(2)}) async-start(bf16[16,256,128]{2,1,0:T(8,128)(2,1)} %bitcast.2), calls=%async_computation.1 | async-start | bytes 2097152 | tf_op jit(solution)/shard_map/all_to_all | solution.py:395
  33.3 10.8 %psum.7.parts_ref = f32[8,128]{1,0:T(8,128)S(1)} all-reduce(f32[8,128]{1,0:T(8,128)S(1)} %get-tuple-element.19), channel_id=1, replica_groups=mesh['dp_0'=4,'dp_1'=2,'tensor_0'=4,'tensor_1'=4] {'dp_0'}, use_global_device_ids=true, to_apply=%region_0.0 | all-reduce | flops 1024 | bytes 8192 | tf_op jit(solution)/shard_map/psum | solution.py:426
  44.1 0.0 copy-start.5
  44.1 0.1 collective-permute-start
  44.1 5.1 %turn_moment.1 = (f32[2,512,512]{2,1,0:T(8,128)}, bf16[2,512,512]{2,1,0:T(8,128)(2,1)}) custom-call(bf16[2,512,512]{2,1,0:T(8,128)(2,1)} %left_ref.4, bf16[2,512,512]{2,1,0:T(8,128)(2,1)} %right_ref.4, f32[2,512,512]{2,1,0:T(8,128)} %moment_ref.3), custom_call_target="tpu_custom_call" | custom-call | tf_op jit(solution)/shard_map/turn_moment/pallas_call | solution.py:191
  49.3 0.0 copy-done
  49.3 0.0 copy-done.5
  49.3 0.0 collective-permute-done.other_ref
  49.3 0.0 copy-start.6
  49.3 0.0 all-to-all-done.1.arrived_ref
  49.3 0.6 copy-done.6
  49.9 10.2 %main_step.1 = (f32[2,512,512]{2,1,0:T(8,128)}, bf16[16,256,128]{2,1,0:T(8,128)(2,1)}, bf16[2,16,32,512]{3,2,1,0:T(8,128)(2,1)}, f32[8,128]{1,0:T(8,128)}) custom-call(s32[128]{0:T(128)} %copy-done, f32[8,128]{1,0:T(8,128)} %copy-done.5, f32[8,128]{1,0:T(8,128)} %copy-done.6, bf16[16,256,128]{2,1,0:T(8,128)(2,1)} %all-to-all-done.1.arrived_ref, ...), custom_call_target="tpu_custom_call" | custom-call | tf_op jit(solution)/shard_map/main_step/pallas_call | solution.py:282
  60.1 0.0 copy-start.4
  60.1 7.2 %all-to-all-start.2 = ((bf16[16,256,128]{2,1,0:T(8,128)(2,1)}), bf16[16,256,128]{2,1,0:T(8,128)(2,1)S(1)}, u32[]{:S(2)}, u32[]{:S(2)}) async-start(bf16[16,256,128]{2,1,0:T(8,128)(2,1)} %get-tuple-element.23), calls=%async_computation.2 | async-start | bytes 2097152 | tf_op jit(solution)/shard_map/all_to_all | solution.py:395
  67.3 0.0 copy-done.4
  67.3 0.0 copy-start.1
  67.3 1.0 convert_element_type.10
  68.4 17.4 %all-to-all-done.2 = bf16[16,256,128]{2,1,0:T(8,128)(2,1)S(1)} async-done(((bf16[16,256,128]{2,1,0:T(8,128)(2,1)}), bf16[16,256,128]{2,1,0:T(8,128)(2,1)S(1)}, u32[]{:S(2)}, u32[]{:S(2)}) %all-to-all-start.2) | async-done | bytes 1048608 | tf_op jit(solution)/shard_map/all_to_all | solution.py:395
  85.8 4.3 %all-to-all-start.4 = ((f16[16,32,896]{2,1,0:T(8,128)(2,1)}), f16[16,32,896]{2,1,0:T(8,128)(2,1)}, u32[]{:S(2)}, u32[]{:S(2)}) async-start(f16[16,32,896]{2,1,0:T(8,128)(2,1)} %convert_element_type.10), calls=%async_computation.4 | async-start | bytes 1835008 | tf_op jit(solution)/shard_map/all_to_all | solution.py:395
  90.1 0.0 copy-done.1
  90.1 1.6 %place_tiles.1.update_ref = bf16[16,32,896]{2,1,0:T(8,128)(2,1)} custom-call(s32[128]{0:T(128)S(1)} %copy-done.1, bf16[128,32,128]{2,1,0:T(8,128)(2,1)S(1)} %bitcast.6), custom_call_target="tpu_custom_call" | custom-call | tf_op jit(solution)/shard_map/place_tiles/pallas_call | solution.py:359
  91.7 13.0 %all-to-all-done.4 = f16[16,32,896]{2,1,0:T(8,128)(2,1)} async-done(((f16[16,32,896]{2,1,0:T(8,128)(2,1)}), f16[16,32,896]{2,1,0:T(8,128)(2,1)}, u32[]{:S(2)}, u32[]{:S(2)}) %all-to-all-start.4) | async-done | bytes 917536 | tf_op jit(solution)/shard_map/all_to_all | solution.py:395
  104.7 3.6 %all-to-all-start.3 = ((bf16[16,32,896]{2,1,0:T(8,128)(2,1)}), bf16[16,32,896]{2,1,0:T(8,128)(2,1)S(1)}, u32[]{:S(2)}, u32[]{:S(2)}) async-start(bf16[16,32,896]{2,1,0:T(8,128)(2,1)} %place_tiles.1.update_ref), calls=%async_computation.3 | async-start | bytes 1835008 | tf_op jit(solution)/shard_map/all_to_all | solution.py:395
  108.4 2.6 %convert_element_type.11.fast_ref = f32[16,32,896]{2,1,0:T(8,128)} convert(f16[16,32,896]{2,1,0:T(8,128)(2,1)} %all-to-all-done.4) | non-fusion elementwise | flops 458752 | bytes 2752512 | tf_op jit(solution)/shard_map/convert_element_type | solution.py:438
  111.0 6.6 %statistics.1 = (f32[2,512,512]{2,1,0:T(8,128)}, f32[2,512,512]{2,1,0:T(8,128)}, f32[2,512,512]{2,1,0:T(8,128)}) custom-call(s32[128]{0:T(128)} %copy-done, f32[8,128]{1,0:T(8,128)} %get-tuple-element.26.scale_ref, bf16[2,512,512]{2,1,0:T(8,128)(2,1)} %bitcast.10, f32[2,512,512]{2,1,0:T(8,128)} %left_ref.5, f32[2,512,512]{2,1,0:T(8,128)} %right_ref.5, ...), custom_call_target="tpu_custom_call" | custom-call | tf_op jit(solution)/shard_map/statistics/pallas_call | solution.py:325
  117.6 4.2 %pull_slow.1 = f32[32,14336]{1,0:T(8,128)} custom-call(f32[32,14336]{1,0:T(8,128)} %slow_ref.1, f32[16,32,896]{2,1,0:T(8,128)} %convert_element_type.11.fast_ref, bf16[16,32,896]{2,1,0:T(8,128)(2,1)} %place_tiles.1.update_ref), custom_call_target="tpu_custom_call" | custom-call | tf_op jit(solution)/shard_map/pull_slow/pallas_call | solution.py:383
  121.8 0.8 all-to-all-done.3
  122.6 1.5 %multiply_subtract_fusion = f32[16,32,896]{2,1,0:T(8,128)} fusion(f32[16,32,896]{2,1,0:T(8,128)S(1)} %bitcast.8, bf16[16,32,896]{2,1,0:T(8,128)(2,1)S(1)} %all-to-all-done.3), kind=kLoop, calls=%fused_computation | loop fusion | flops 1376256 | bytes 4587520 | tf_op jit(solution)/shard_map/sub | solution.py:447
Async XLA Ops:
  0.6 10.2 %copy-start.2 = (s32[8,112]{1,0:T(8,128)S(1)}, s32[8,112]{1,0:T(8,128)}, u32[]{:S(2)}) copy-start(s32[8,112]{1,0:T(8,128)} %tb.1) | copy-start | bytes 10756
  0.6 10.2 %copy-start.3 = (s32[224]{0:T(256)S(1)}, s32[224]{0:T(256)}, u32[]{:S(2)}) copy-start(s32[224]{0:T(256)} %owner.1) | copy-start | bytes 2692
  2.8 24.5 %all-to-all-start = ((bf16[16,232,128]{2,1,0:T(8,128)(2,1)}), bf16[16,232,128]{2,1,0:T(8,128)(2,1)S(1)}, u32[]{:S(2)}, u32[]{:S(2)}) async-start(bf16[16,232,128]{2,1,0:T(8,128)(2,1)} %cut_tiles.1), calls=%async_computation | async-start | bytes 1900544 | tf_op jit(solution)/shard_map/all_to_all | solution.py:395
  14.0 35.3 %copy-start = (s32[128]{0:T(128)}, s32[128]{0:T(128)S(1)}, u32[]{:S(2)}) copy-start(s32[128]{0:T(128)S(1)} %tables.1.tab) | copy-start | bytes 1540
  29.0 20.4 %all-to-all-start.1 = ((bf16[16,256,128]{2,1,0:T(8,128)(2,1)}), bf16[16,256,128]{2,1,0:T(8,128)(2,1)}, u32[]{:S(2)}, u32[]{:S(2)}) async-start(bf16[16,256,128]{2,1,0:T(8,128)(2,1)} %bitcast.2), calls=%async_computation.1 | async-start | bytes 2097152 | tf_op jit(solution)/shard_map/all_to_all | solution.py:395
  44.1 5.2 %copy-start.5 = (f32[8,128]{1,0:T(8,128)}, f32[8,128]{1,0:T(8,128)S(1)}, u32[]{:S(2)}) copy-start(f32[8,128]{1,0:T(8,128)S(1)} %psum.7.parts_ref) | copy-start | bytes 12292
  44.1 5.2 %collective-permute-start = (f32[8,128]{1,0:T(8,128)S(1)}, f32[8,128]{1,0:T(8,128)S(1)}, u32[]{:S(2)}, u32[]{:S(2)}) collective-permute-start(f32[8,128]{1,0:T(8,128)S(1)} %psum.7.parts_ref), channel_id=1, source_target_pairs={{0,16},{16,0},{1,17},{17,1},{2,18},{18,2},{3,19},{19,3},{4,20},{20... | collective-permute-start | bytes 12296 | tf_op jit(solution)/shard_map/ppermute | solution.py:428
  49.3 0.6 copy-start.6
  60.1 7.2 %copy-start.4 = (f32[512,896]{1,0:T(8,128)S(1)}, f32[512,896]{1,0:T(8,128)}, u32[]{:S(2)}) copy-start(f32[512,896]{1,0:T(8,128)} %param.14) | copy-start | bytes 5505028
  60.1 25.7 %all-to-all-start.2 = ((bf16[16,256,128]{2,1,0:T(8,128)(2,1)}), bf16[16,256,128]{2,1,0:T(8,128)(2,1)S(1)}, u32[]{:S(2)}, u32[]{:S(2)}) async-start(bf16[16,256,128]{2,1,0:T(8,128)(2,1)} %get-tuple-element.23), calls=%async_computation.2 | async-start | bytes 2097152 | tf_op jit(solution)/shard_map/all_to_all | solution.py:395
  67.3 22.8 %copy-start.1 = (s32[128]{0:T(128)S(1)}, s32[128]{0:T(128)}, u32[]{:S(2)}) copy-start(s32[128]{0:T(128)} %copy-done) | copy-start | bytes 1540
  85.8 18.9 %all-to-all-start.4 = ((f16[16,32,896]{2,1,0:T(8,128)(2,1)}), f16[16,32,896]{2,1,0:T(8,128)(2,1)}, u32[]{:S(2)}, u32[]{:S(2)}) async-start(f16[16,32,896]{2,1,0:T(8,128)(2,1)} %convert_element_type.10), calls=%async_computation.4 | async-start | bytes 1835008 | tf_op jit(solution)/shard_map/all_to_all | solution.py:395
  104.7 17.9 %all-to-all-start.3 = ((bf16[16,32,896]{2,1,0:T(8,128)(2,1)}), bf16[16,32,896]{2,1,0:T(8,128)(2,1)S(1)}, u32[]{:S(2)}, u32[]{:S(2)}) async-start(bf16[16,32,896]{2,1,0:T(8,128)(2,1)} %place_tiles.1.update_ref), calls=%async_computation.3 | async-start | bytes 1835008 | tf_op jit(solution)/shard_map/all_to_all | solution.py:395
